TPU v7x, 8 devices: a whole 2x2x1 slice. The times are simulated.
8 devices in a mesh: dp: 1 (over z), sp: 2 (over y), tp: 4 (over x, core).
Axes of the slice: x: 2, y: 2, z: 1, core: 2. Of those that a mesh axis runs over, the one named last changes fastest.
Arguments:
- hidden: bfloat16 [256, 2048], P('dp')
- new_pos: int32 [256], P('dp')
- k_self: bfloat16 [256, 256, 8, 128], P('dp', 'sp', 'tp')
- v_self: bfloat16 [256, 256, 8, 128], P('dp', 'sp', 'tp')
- k_cross: bfloat16 [256, 512, 8, 128], P('dp', None, 'tp')
- v_cross: bfloat16 [256, 512, 8, 128], P('dp', None, 'tp')
- xvalid: int32 [256, 512], P('dp')
- rowmask: int32 [256], P('dp')
- self_attn_norm: bfloat16 [2048], replicated
- self_wq: bfloat16 [2048, 2048], P(None, 'tp')
- self_wk: bfloat16 [2048, 1024], P(None, 'tp')
- self_wv: bfloat16 [2048, 1024], P(None, 'tp')
- self_wo: bfloat16 [2048, 2048], P('tp')
- self_mlp_norm: bfloat16 [2048], replicated
- self_wgate: bfloat16 [2048, 6144], P(None, 'tp')
- self_wup: bfloat16 [2048, 6144], P(None, 'tp')
- self_wdown: bfloat16 [6144, 2048], P('tp')
- cross_attn_norm: bfloat16 [2048], replicated
- cross_wq: bfloat16 [2048, 2048], P(None, 'tp')
- cross_qnorm: bfloat16 [128], replicated
- cross_wo: bfloat16 [2048, 2048], P('tp')
- cross_gates: float32 [2], replicated
- cross_mlp_norm: bfloat16 [2048], replicated
- cross_wgate: bfloat16 [2048, 6144], P(None, 'tp')
- cross_wup: bfloat16 [2048, 6144], P(None, 'tp')
- cross_wdown: bfloat16 [6144, 2048], P('tp')
Outputs:
- output 1: bfloat16 [256, 2048], P('dp')
- output 2: bfloat16 [256, 256, 8, 128], P('dp', 'sp', 'tp')
- output 3: bfloat16 [256, 256, 8, 128], P('dp', 'sp', 'tp')
All inputs are finite; a program needn't handle non-finite values.
Results may differ from a plain program's by a relative error of at most 0.0146321.
Values sent between devices are 32-bit elements.
A program may use at most 1 GiB of HBM per device.

v0:
```python
import math
import jax
import jax.numpy as jnp
from jax import lax
from jax.sharding import PartitionSpec as P

NORM_EPS = 1e-5
ROPE_THETA = 500000.0
ROPE_FACTOR = 8.0
LOW_FREQ = 1.0
HIGH_FREQ = 4.0
ORIG_CTX = 8192.0
NEG_BIG = -1e30


def rope_freqs(head_dim):
    inv_freq = 1.0 / (ROPE_THETA ** (jnp.arange(0, head_dim, 2).astype(jnp.float32) / head_dim))
    wavelen = 2.0 * math.pi / inv_freq
    smooth = (ORIG_CTX / wavelen - LOW_FREQ) / (HIGH_FREQ - LOW_FREQ)
    mid_freq = (1.0 - smooth) * inv_freq / ROPE_FACTOR + smooth * inv_freq
    scaled = jnp.where(wavelen > ORIG_CTX / LOW_FREQ, inv_freq / ROPE_FACTOR, mid_freq)
    return jnp.where(wavelen < ORIG_CTX / HIGH_FREQ, inv_freq, scaled)


def apply_rope(vectors, positions):
    head_dim = vectors.shape[-1]
    half_dim = head_dim // 2
    angles = positions.astype(jnp.float32)[:, None] * rope_freqs(head_dim)[None, :]
    cos_t = jnp.cos(angles)[:, None, :]
    sin_t = jnp.sin(angles)[:, None, :]
    first_half = vectors[..., :half_dim]
    second_half = vectors[..., half_dim:]
    return jnp.concatenate([first_half * cos_t - second_half * sin_t, second_half * cos_t + first_half * sin_t], axis=-1)


def rms_norm(values, gain_vec):
    vals32 = values.astype(jnp.float32)
    inv_rms = lax.rsqrt(jnp.mean(vals32 * vals32, axis=-1, keepdims=True) + NORM_EPS)
    return (vals32 * inv_rms * gain_vec.astype(jnp.float32)).astype(jnp.bfloat16)


def mlp_partial(normed, w_gate, w_up, w_down):
    gate_val = jnp.dot(normed, w_gate, preferred_element_type=jnp.float32).astype(jnp.bfloat16)
    up_val = jnp.dot(normed, w_up, preferred_element_type=jnp.float32).astype(jnp.bfloat16)
    hidden_act = (jax.nn.silu(gate_val.astype(jnp.float32)) * up_val.astype(jnp.float32)).astype(jnp.bfloat16)
    return jnp.dot(hidden_act, w_down, preferred_element_type=jnp.float32)


def local_softmax(queries, key_rows, val_rows, valid_mask, score_scale):
    scores = jnp.einsum('bkgd,btkd->bkgt', queries, key_rows, preferred_element_type=jnp.float32) * score_scale
    scores = jnp.where(valid_mask, scores, NEG_BIG)
    part_max = jnp.max(scores, axis=-1)
    probs_loc = jnp.where(valid_mask, jnp.exp(scores - part_max[..., None]), 0.0)
    part_sum = jnp.sum(probs_loc, axis=-1)
    part_out = jnp.einsum('bkgt,btkd->bkgd', probs_loc.astype(jnp.bfloat16), val_rows, preferred_element_type=jnp.float32)
    return part_max, part_sum, part_out


def combine_sp(part_max, part_sum, part_out):
    glob_max = lax.pmax(part_max, 'sp')
    factor = jnp.exp(part_max - glob_max)
    total_sum = lax.psum(part_sum * factor, 'sp')
    total_out = lax.psum(part_out * factor[..., None], 'sp')
    return total_out / total_sum[..., None]


def solution(mesh):
    cache_spec = P('dp', 'sp', 'tp', None)
    cross_spec = P('dp', None, 'tp', None)
    row_spec = P('dp', None)
    vec_spec = P('dp')
    full_spec = P(None)
    col_spec = P(None, 'tp')
    split_rows = P('tp', None)
    in_specs = (row_spec, vec_spec, cache_spec, cache_spec, cross_spec, cross_spec, row_spec, vec_spec,
                full_spec, col_spec, col_spec, col_spec, split_rows, full_spec, col_spec, col_spec, split_rows,
                full_spec, col_spec, full_spec, split_rows, full_spec, full_spec, col_spec, col_spec, split_rows)
    out_specs = (row_spec, cache_spec, cache_spec)

    def local_step(hidden, new_pos, k_self, v_self, k_cross, v_cross, xvalid, rowmask,
                   self_attn_norm, self_wq, self_wk, self_wv, self_wo, self_mlp_norm,
                   self_wgate, self_wup, self_wdown, cross_attn_norm, cross_wq, cross_qnorm,
                   cross_wo, cross_gates, cross_mlp_norm, cross_wgate, cross_wup, cross_wdown):
        batch_rows = hidden.shape[0]
        len_local = k_self.shape[1]
        kv_local = k_self.shape[2]
        head_dim = k_self.shape[3]
        heads_local = self_wq.shape[1] // head_dim
        group_size = heads_local // kv_local
        score_scale = head_dim ** -0.5
        normed = rms_norm(hidden, self_attn_norm)
        queries = jnp.dot(normed, self_wq, preferred_element_type=jnp.float32).astype(jnp.bfloat16)
        key_new = jnp.dot(normed, self_wk, preferred_element_type=jnp.float32).astype(jnp.bfloat16)
        val_new = jnp.dot(normed, self_wv, preferred_element_type=jnp.float32).astype(jnp.bfloat16)
        queries = apply_rope(queries.reshape(batch_rows, heads_local, head_dim).astype(jnp.float32), new_pos).astype(jnp.bfloat16)
        key_new = apply_rope(key_new.reshape(batch_rows, kv_local, head_dim).astype(jnp.float32), new_pos).astype(jnp.bfloat16)
        val_new = val_new.reshape(batch_rows, kv_local, head_dim)
        local_pos = new_pos - lax.axis_index('sp') * len_local
        slot_ids = jnp.arange(len_local)
        hit_mask = (slot_ids[None, :] == local_pos[:, None])[:, :, None, None]
        k_new_cache = jnp.where(hit_mask, key_new[:, None], k_self)
        v_new_cache = jnp.where(hit_mask, val_new[:, None], v_self)
        seen_mask = (slot_ids[None, :] <= local_pos[:, None])[:, None, None, :]
        self_stats = local_softmax(queries.reshape(batch_rows, kv_local, group_size, head_dim), k_new_cache, v_new_cache, seen_mask, score_scale)
        self_attn = combine_sp(self_stats[0], self_stats[1], self_stats[2])
        self_flat = self_attn.astype(jnp.bfloat16).reshape(batch_rows, heads_local * head_dim)
        attn_sum = lax.psum(jnp.dot(self_flat, self_wo, preferred_element_type=jnp.float32), 'tp')
        after_attn = (hidden.astype(jnp.float32) + attn_sum).astype(jnp.bfloat16)
        mlp_sum = lax.psum(mlp_partial(rms_norm(after_attn, self_mlp_norm), self_wgate, self_wup, self_wdown), 'tp')
        after_mlp = (after_attn.astype(jnp.float32) + mlp_sum).astype(jnp.bfloat16)
        normed = rms_norm(after_mlp, cross_attn_norm)
        cross_q = jnp.dot(normed, cross_wq, preferred_element_type=jnp.float32).astype(jnp.bfloat16)
        cross_q = rms_norm(cross_q.reshape(batch_rows, heads_local, head_dim), cross_qnorm)
        cross_mask = (xvalid > 0)[:, None, None, :]
        cross_stats = local_softmax(cross_q.reshape(batch_rows, kv_local, group_size, head_dim), k_cross, v_cross, cross_mask, score_scale)
        cross_attn = cross_stats[2] / cross_stats[1][..., None]
        cross_flat = cross_attn.astype(jnp.bfloat16).reshape(batch_rows, heads_local * head_dim)
        gate_vals = jnp.tanh(cross_gates.astype(jnp.float32))
        row_scale = rowmask.astype(jnp.float32)[:, None]
        xattn_sum = lax.psum(jnp.dot(cross_flat, cross_wo, preferred_element_type=jnp.float32), 'tp')
        after_cross = (after_mlp.astype(jnp.float32) + gate_vals[0] * row_scale * xattn_sum).astype(jnp.bfloat16)
        xmlp_sum = lax.psum(mlp_partial(rms_norm(after_cross, cross_mlp_norm), cross_wgate, cross_wup, cross_wdown), 'tp')
        after_xmlp = (after_cross.astype(jnp.float32) + gate_vals[1] * row_scale * xmlp_sum).astype(jnp.bfloat16)
        return after_xmlp, k_new_cache, v_new_cache

    return jax.shard_map(local_step, mesh=mesh, in_specs=in_specs, out_specs=out_specs, check_vma=False)
```

profile of v0, /device:TPU:0, one launch (start us, length us, event | category | flops | bytes accessed | tf_op | source)
XLA Modules:
  0.0 431.5 jit_solution(10929859912333581827)
XLA Ops:
  7.2 0.0 all-reduce.6.cloned.1.call-start
  7.2 0.5 compare_select_fusion.1
  7.8 0.7 convert_element_type.158
  8.5 1.5 fusion.17
  10.0 2.3 convolution_convert_fusion.7
  12.4 1.0 multiply_cosine_fusion
  13.4 0.8 copy.56
  14.1 0.8 copy.57
  14.9 0.1 copy.58
  15.1 1.9 convolution_convert_fusion.6
  17.0 0.1 copy.60
  17.1 0.7 iota_compare_fusion.1
  17.8 3.2 fusion.35
  21.0 1.2 reshape.216
  22.2 1.4 subtract_convert_fusion
  23.6 46.0 %broadcast_select_fusion.1 = (bf16[256,128,2,128]{3,2,1,0:T(2,128)(2,1)}, bf16[256,128,2,128]{3,2,1,0:T(2,128)(2,1)}) fusion(bf16[256,128,2,128]{3,2,1,0:T(2,128)(2,1)} %param.28, pred[256,128]{1,0:T(8,128)(4,1)S(1)} %copy-done.6, bf16[256,2,128]{2,1,0:T(2,128)(2,1)S(1)} %copy.58, bf16[256,128,2,128]{3,2,1,0:T(2,128)(2,1)} %param.29, ...), kind=kLoop, calls=%fused_computation.6 | loop fusion | flops 16777216 | bytes 67403776 | tf_op jit(solution)/shard_map/jit(_where)/select_n | solution.py:101
  69.6 12.8 %fusion.84 = (f32[256,2,2]{2,1,0:T(2,128)S(1)}, f32[256,2,2,128]{3,2,1,0:T(2,128)S(1)}) fusion(bf16[256,128,2,128]{3,2,1,0:T(2,128)(2,1)} %get-tuple-element.15, bf16[256,2,2,64]{3,2,1,0:T(2,128)(2,1)S(1)} %bitcast.34, bf16[256,2,2,64]{3,2,1,0:T(2,128)(2,1)S(1)} %bitcast.33, pred[256,128]{1,0:T(8,128)(4,1)S(1)} %copy-done.7), kind=kOutput, calls=%fused_computation.107 | convolution fusion | flops 34470912 | bytes 17600512 | tf_op jit(solution)/shard_map/bkgd,btkd->bkgt/dot_general | solution.py:50
  82.4 13.4 %pmax.7 = f32[256,2,2]{2,1,0:T(2,128)S(1)} all-reduce(f32[256,2,2]{2,1,0:T(2,128)S(1)} %get-tuple-element.27), channel_id=1, replica_groups=mesh['dp'=1,'sp'=2,'tp'=4] {'sp'}, use_global_device_ids=true, to_apply=%region_2.3 | all-reduce | flops 1024 | bytes 8192 | tf_op jit(solution)/shard_map/pmax | solution.py:60
  95.9 1.4 fusion.70
  97.3 0.1 fusion.81
  97.4 12.0 %fusion.46 = f32[256,2,2,128]{3,2,1,0:T(2,128)} fusion(bf16[256,128,2,128]{3,2,1,0:T(2,128)(2,1)} %get-tuple-element.16, f32[256,2,2]{2,1,0:T(2,128)S(1)} %bitcast.35, f32[256,2,2,128]{3,2,1,0:T(2,128)S(1)} %get-tuple-element.28, pred[256,128]{1,0:T(8,128)(4,1)S(1)} %copy-done.7, f32[256,2,2]{2,1,0:T(2,128)S(1)} %get-tuple-element.27), kind=kOutput, calls=%fused_computation.60 | convolution fusion | flops 34078720 | bytes 17866752 | tf_op jit(solution)/shard_map/bkgt,btkd->bkgd/dot_general | solution.py:55
  109.4 0.0 all-reduce.8.cloned.1.call-start
  109.5 14.7 %psum.43 = f32[256,2,2]{2,1,0:T(2,128)S(1)} all-reduce(f32[256,2,2]{2,1,0:T(2,128)S(1)} %bitcast.30), channel_id=1, replica_groups=mesh['dp'=1,'sp'=2,'tp'=4] {'sp'}, use_global_device_ids=true, to_apply=%region_5.6 | all-reduce | flops 1024 | bytes 8192 | tf_op jit(solution)/shard_map/psum | solution.py:62
  124.1 11.6 %all-reduce.6.cloned.1.call-done = f32[256,2,2,128]{3,2,1,0:T(2,128)} async-done(((f32[256,2,2,128]{3,2,1,0:T(2,128)}), f32[256,2,2,128]{3,2,1,0:T(2,128)}) %all-reduce.6.cloned.1.call-update) | async-done | bytes 524304 | tf_op jit(solution)/shard_map/psum | solution.py:63
  135.7 1.7 divide_convert_fusion
  137.4 0.1 reshape.214
  137.5 2.0 fusion.87
  139.5 0.0 all-reduce.8.cloned.1.call-update
  139.5 0.0 all-reduce.10.cloned.1.call-start
  139.6 0.6 copy-done.8
  140.2 45.1 %all-reduce.8.cloned.1.call-done = f32[256,2048]{1,0:T(8,128)} async-done(((f32[256,2048]{1,0:T(8,128)}), f32[256,2048]{1,0:T(8,128)}) %all-reduce.8.cloned.1.call-update) | async-done | bytes 2097168 | tf_op jit(solution)/shard_map/psum | solution.py:107
  185.3 2.0 fusion.21
  187.3 5.8 %fusion.16 = f32[256,1536]{1,0:T(8,128)} fusion(bf16[2048,1536]{1,0:T(8,128)(2,1)} %param.40, bf16[256,2048]{1,0:T(8,128)(2,1)S(1)} %get-tuple-element.8, f32[2048]{0:T(1024)S(1)} %convert_element_type.173, f32[256]{0:T(256)S(1)} %add_rsqrt_fusion.3), kind=kOutput, calls=%fused_computation.34 | convolution fusion | flops 1613496320 | bytes 8922112 | tf_op jit(solution)/shard_map/dot_general | solution.py:43
  193.1 10.0 %fusion.56 = f32[256,2048]{1,0:T(8,128)} fusion(bf16[1536,2048]{1,0:T(8,128)(2,1)} %param.42, bf16[2048,1536]{1,0:T(8,128)(2,1)} %param.41, f32[256,1536]{1,0:T(8,128)} %fusion.16, bf16[256,2048]{1,0:T(8,128)(2,1)S(1)} %get-tuple-element.8, f32[2048]{0:T(1024)S(1)} %convert_element_type.173, f32[256]{0:T(256)S(1)} %add_rsqrt_fusion.3), kind=kOutput, calls=%fused_computation.67 | convolution fusion | flops 3226468352 | bytes 17310720 | tf_op jit(solution)/shard_map/dot_general | solution.py:46
  203.1 0.0 all-reduce.10.cloned.1.call-update
  203.1 0.0 all-reduce.12.cloned.1.call-start
  203.2 0.6 copy-done.9
  203.8 0.4 copy-done.5
  204.2 0.1 broadcast_compare_fusion
  204.2 44.8 %all-reduce.10.cloned.1.call-done = f32[256,2048]{1,0:T(8,128)} async-done(((f32[256,2048]{1,0:T(8,128)}), f32[256,2048]{1,0:T(8,128)}) %all-reduce.10.cloned.1.call-update) | async-done | bytes 2097168 | tf_op jit(solution)/shard_map/psum | solution.py:109
  249.0 2.1 fusion.25
  251.1 0.1 copy-done.13
  251.2 0.8 fusion.85
  252.0 0.2 mul.321
  252.2 0.3 reduce_sum.67
  252.6 0.2 reshape.219
  252.7 0.3 reshape.218
  253.1 26.4 %multiply_select_fusion = f32[256,2,2,512]{3,2,1,0:T(2,128)S(1)} fusion(pred[256,512]{1,0:T(8,128)(4,1)S(1)} %broadcast_compare_fusion, bf16[256,512,2,128]{3,2,1,0:T(2,128)(2,1)} %param.30, f32[256,2,2,128]{3,2,1,0:T(2,128)S(1)} %reshape.218, f32[128]{0:T(128)S(1)} %convert_element_type.189, f32[256,2,2]{2,1,0:T(2,128)S(1)} %reshape.219), kind=kOutput, calls=%fused_computation.52 | convolution fusion | flops 135659520 | bytes 69865984 | tf_op jit(solution)/shard_map/bkgd,btkd->bkgt/dot_general | solution.py:50
  279.5 4.0 fusion.86
  283.4 26.3 %fusion.40 = bf16[256,2,2,128]{3,2,1,0:T(2,128)(2,1)S(1)} fusion(bf16[256,512,2,128]{3,2,1,0:T(2,128)(2,1)} %param.31, bf16[256,2,2,512]{3,2,1,0:T(2,128)(2,1)} %get-tuple-element.32, f32[256,2,2]{2,1,0:T(2,128)S(1)} %get-tuple-element.31), kind=kOutput, calls=%fused_computation.58 | convolution fusion | flops 134479872 | bytes 68423680 | tf_op jit(solution)/shard_map/bkgt,btkd->bkgd/dot_general | solution.py:55
  309.7 0.1 reshape.215
  309.8 3.6 fusion.88
  313.5 0.0 all-reduce.12.cloned.1.call-update
  313.5 0.3 all-reduce.14.cloned.1.call-start
  313.8 0.3 copy-done.15
  314.1 0.0 copy-done.10
  314.2 0.6 fusion.83
  314.7 1.3 convert_multiply_fusion.8
  316.0 43.4 %all-reduce.12.cloned.1.call-done = f32[256,2048]{1,0:T(8,128)} async-done(((f32[256,2048]{1,0:T(8,128)}), f32[256,2048]{1,0:T(8,128)}) %all-reduce.12.cloned.1.call-update) | async-done | bytes 2097168 | tf_op jit(solution)/shard_map/psum | solution.py:120
  359.4 2.1 fusion.29
  361.5 4.6 %fusion.12 = f32[256,1536]{1,0:T(8,128)S(1)} fusion(bf16[2048,1536]{1,0:T(8,128)(2,1)} %param.49, bf16[256,2048]{1,0:T(8,128)(2,1)S(1)} %get-tuple-element.4, f32[2048]{0:T(1024)S(1)} %convert_element_type.195, f32[256]{0:T(256)S(1)} %add_rsqrt_fusion.1), kind=kOutput, calls=%fused_computation.28 | convolution fusion | flops 1613496320 | bytes 8922112 | tf_op jit(solution)/shard_map/dot_general | solution.py:43
  366.1 9.4 %fusion.57 = f32[256,2048]{1,0:T(8,128)} fusion(bf16[1536,2048]{1,0:T(8,128)(2,1)} %param.51, bf16[2048,1536]{1,0:T(8,128)(2,1)} %param.50, f32[256,1536]{1,0:T(8,128)S(1)} %fusion.12, bf16[256,2048]{1,0:T(8,128)(2,1)S(1)} %get-tuple-element.4, f32[2048]{0:T(1024)S(1)} %convert_element_type.195, f32[256]{0:T(256)S(1)} %add_rsqrt_fusion.1), kind=kOutput, calls=%fused_computation.68 | convolution fusion | flops 3226468352 | bytes 17310720 | tf_op jit(solution)/shard_map/dot_general | solution.py:46
  375.6 45.9 %all-reduce.14.cloned.1.call-done = f32[256,2048]{1,0:T(8,128)} async-done(((f32[256,2048]{1,0:T(8,128)}), f32[256,2048]{1,0:T(8,128)}) %all-reduce.14.cloned.1.call-update) | async-done | bytes 2097168 | tf_op jit(solution)/shard_map/psum | solution.py:122
  421.5 3.0 fusion.32
  (42 shorter events, 0.2 us)
Async XLA Ops:
  7.2 130.3 %copy-start = (bf16[512,2048]{1,0:T(8,128)(2,1)S(1)}, bf16[512,2048]{1,0:T(8,128)(2,1)}, u32[]{:S(2)}) copy-start(bf16[512,2048]{1,0:T(8,128)(2,1)} %param.38) | copy-start | bytes 6291460
  7.2 128.5 %all-reduce.6.cloned.1.call-start = ((), (), s32[]{:S(2)}) async-start(), calls=%async_computation | async-start | bytes 1048576 | tf_op jit(solution)/shard_map/psum | solution.py:63
  8.5 3.9 copy-start.11
  10.0 5.0 %copy-start.2 = (bf16[256,2048]{1,0:T(8,128)(2,1)S(1)}, bf16[256,2048]{1,0:T(8,128)(2,1)}, u32[]{:S(2)}) copy-start(bf16[256,2048]{1,0:T(8,128)(2,1)} %param.26) | copy-start | bytes 3145732
  17.8 4.4 %copy-start.4 = (f32[256,64]{1,0:T(8,128)S(1)}, f32[256,64]{1,0:T(8,128)}, u32[]{:S(2)}) copy-start(f32[256,64]{1,0:T(8,128)} %copy.56) | copy-start | bytes 196612
  21.0 2.6 copy-start.6
  23.6 46.0 %copy-start.7 = (pred[256,128]{1,0:T(8,128)(4,1)S(1)}, pred[256,128]{1,0:T(8,128)(4,1)}, u32[]{:S(2)}) copy-start(pred[256,128]{1,0:T(8,128)(4,1)} %get-tuple-element.21) | copy-start | bytes 98308
  109.4 75.9 %all-reduce.8.cloned.1.call-start = ((), (), s32[]{:S(2)}) async-start(), calls=%async_computation.1 | async-start | bytes 4194304 | tf_op jit(solution)/shard_map/psum | solution.py:107
  139.5 0.7 copy-start.8
  139.5 45.8 %copy-start.3 = (bf16[256,2048]{1,0:T(8,128)(2,1)S(1)}, bf16[256,2048]{1,0:T(8,128)(2,1)}, u32[]{:S(2)}) copy-start(bf16[256,2048]{1,0:T(8,128)(2,1)} %param.26) | copy-start | bytes 3145732
  139.5 109.4 %all-reduce.10.cloned.1.call-start = ((), (), s32[]{:S(2)}) async-start(), calls=%async_computation.2 | async-start | bytes 4194304 | tf_op jit(solution)/shard_map/psum | solution.py:109
  203.1 0.7 copy-start.9
  203.1 0.7 copy-start.14
  203.1 1.1 copy-start.5
  203.1 156.3 %all-reduce.12.cloned.1.call-start = ((), (), s32[]{:S(2)}) async-start(), calls=%async_computation.3 | async-start | bytes 4194304 | tf_op jit(solution)/shard_map/psum | solution.py:120
  249.0 2.2 copy-start.13
  313.4 0.7 copy-start.15
  313.5 0.7 copy-start.10
  313.5 1.3 copy-start.12
  313.5 108.0 %all-reduce.14.cloned.1.call-start = ((), (), s32[]{:S(2)}) async-start(), calls=%async_computation.4 | async-start | bytes 4194304 | tf_op jit(solution)/shard_map/psum | solution.py:122
  421.5 3.0 copy-start.1
Sparse Core Ops, SparseCore 0:
  109.5 26.1 all-reduce.5
  139.7 45.6 all-reduce.7
  203.2 45.7 all-reduce.9
  313.6 45.7 all-reduce.11
  375.7 45.7 all-reduce.13
where the time goes:
time: 439 us; the launch traced here: 431 us
  waiting for transfers between devices  191 us (44%)
  matrix products  121 us (28%)
  other arithmetic  70 us (16%)
  blocking collectives  28.1 us (6%)
  between operations  14.5 us (3%)
  local copies, waits for them, and re-layouts  6.56 us (1%)
    select_n x1, other arithmetic, local_step(): k_new_cache = jnp.where(hit_mask, key_new[:, None], k_self)  46 us
    psum x1, waiting for transfers between devices, local_step(): lax.psum(mlp_partial(rms_norm(after_cross, cross_mlp_norm), cross_wgate,...  45.9 us
    psum x1, waiting for transfers between devices, local_step(): lax.psum(jnp.dot(self_flat, self_wo, preferred_element_type=jnp.float32),...  45.1 us
    psum x1, waiting for transfers between devices, local_step(): lax.psum(mlp_partial(rms_norm(after_attn, self_mlp_norm), self_wgate, sel...  44.8 us
    psum x1, waiting for transfers between devices, local_step(): lax.psum(jnp.dot(cross_flat, cross_wo, preferred_element_type=jnp.float32...  43.4 us
    dot_general x2, matrix products, local_softmax(): jnp.einsum('bkgd,btkd->bkgt', queries, key_rows, preferred_element_type=j...  39.2 us
    dot_general x2, matrix products, local_softmax(): jnp.einsum('bkgt,btkd->bkgd', probs_loc.astype(jnp.bfloat16), val_rows, p...  38.3 us
    dot_general x2, matrix products, mlp_partial(): return jnp.dot(hidden_act, w_down, preferred_element_type=jnp.float32)  19.4 us
  transfers between devices with their start and end apart: 5, of which 5 were waited for; matrix products, arithmetic and copies ran while one was open for 0% of the time, Pallas kernels for 0%

commit v1 on v0

v1 whole, which is shorter than its diff:
```python
import functools
import math
import jax
import jax.numpy as jnp
from jax import lax
from jax.experimental import pallas as pl
from jax.experimental.pallas import tpu as pltpu
from jax.sharding import PartitionSpec as P

NORM_EPS = 1e-5
ROPE_THETA = 500000.0
ROPE_FACTOR = 8.0
LOW_FREQ = 1.0
HIGH_FREQ = 4.0
ORIG_CTX = 8192.0
NEG_BIG = -1e30

BF = jnp.bfloat16
F32 = jnp.float32
D = 128
HL = 4
KL = 2
NB = 256
NH = 128
NQ = 64
HID = 2048
NCH = 4
W = HID // NCH
VMEM_MAX = 66 * 1024 * 1024 - 2 * 1024 * 1024
MESH = pl.DeviceIdType.MESH
ANY = pl.BlockSpec(memory_space=pl.ANY)
VM = pl.BlockSpec(memory_space=pltpu.VMEM)


def rope_freqs(head_dim):
    inv_freq = 1.0 / (ROPE_THETA ** (jnp.arange(0, head_dim, 2).astype(jnp.float32) / head_dim))
    wavelen = 2.0 * math.pi / inv_freq
    smooth = (ORIG_CTX / wavelen - LOW_FREQ) / (HIGH_FREQ - LOW_FREQ)
    mid_freq = (1.0 - smooth) * inv_freq / ROPE_FACTOR + smooth * inv_freq
    scaled = jnp.where(wavelen > ORIG_CTX / LOW_FREQ, inv_freq / ROPE_FACTOR, mid_freq)
    return jnp.where(wavelen < ORIG_CTX / HIGH_FREQ, inv_freq, scaled)


def norm32(vals32, gain32):
    inv = lax.rsqrt(jnp.mean(vals32 * vals32, axis=-1, keepdims=True) + NORM_EPS)
    return (vals32 * inv * gain32).astype(BF)


def dot(a, b):
    return jnp.dot(a, b, preferred_element_type=F32)


def dot_nt(a, b):
    return lax.dot_general(a, b, (((1,), (1,)), ((), ())), preferred_element_type=F32)


def pair_attend(lhs, keys, vals, valid, scale):
    s = dot_nt(lhs, keys) * scale
    s = jnp.where(valid, s, NEG_BIG)
    m = jnp.max(s, axis=-1, keepdims=True)
    p = jnp.where(valid, jnp.exp(s - m), 0.0)
    l = jnp.sum(p, axis=-1, keepdims=True)
    o = dot(p.astype(BF), vals)
    first = lax.broadcasted_iota(jnp.int32, (8, D), 0) < HL
    return m, l, jnp.where(first, o[:, :D], o[:, D:])


def spread_heads(ref, heads, start, rows):
    odd = (lax.broadcasted_iota(jnp.int32, (rows, D), 0) % 2) == 1
    for h in range(HL):
        ref[pl.ds(start * 8 + h, rows, stride=8), :] = jnp.where(odd, 0.0, heads[h])
        ref[pl.ds(start * 8 + HL + h, rows, stride=8), :] = jnp.where(odd, heads[h], 0.0)


SR = 16


def self_kernel(pos_ref, hid_ref, g_ref, wq_ref, wk_ref, wv_ref, cos_ref, sin_ref, k_ref, v_ref,
                ko_ref, vo_ref, o_ref, st_ref, qs, kn, vn):
    step = pl.program_id(0)

    @pl.when(step == 0)
    def _():
        x = norm32(hid_ref[...].astype(F32), g_ref[...].astype(F32))
        cos, sin = cos_ref[...], sin_ref[...]

        def rope(part):
            part = part.astype(BF).astype(F32)
            return (part * cos + pltpu.roll(part, D // 2, 1) * sin).astype(BF).astype(F32)

        q = dot(x, wq_ref[...])
        spread_heads(qs, [rope(q[:, h * D:(h + 1) * D]) for h in range(HL)], 0, NB)
        k = dot(x, wk_ref[...])
        v = dot(x, wv_ref[...])
        for h in range(KL):
            kn[pl.ds(h, NB, stride=KL), :] = rope(k[:, h * D:(h + 1) * D])
            vn[pl.ds(h, NB, stride=KL), :] = v[:, h * D:(h + 1) * D].astype(BF).astype(F32)

    T2 = k_ref.shape[1]
    scale = D ** -0.5
    col = lax.broadcasted_iota(jnp.int32, (8, T2), 1)
    row = lax.broadcasted_iota(jnp.int32, (8, T2), 0)
    tok = col // KL
    head_ok = (col % KL) == ((row % HL) // (HL // KL))
    lane = lax.broadcasted_iota(jnp.int32, (8, D), 1)
    i16 = lax.broadcasted_iota(jnp.int32, (16, D), 0)

    def patch(new_ref, dst_ref, r, b, lp):
        base = pl.multiple_of((jnp.clip(lp, 0, T2 // KL - 1) // 8) * 16, 16)
        fresh = jnp.where(i16 % 2 == 0, new_ref[pl.ds(2 * b, 1), :], new_ref[pl.ds(2 * b + 1, 1), :])
        old = dst_ref[r, pl.ds(base, 16), :].astype(F32)
        dst_ref[r, pl.ds(base, 16), :] = jnp.where(base + i16 - i16 % 2 == 2 * lp, fresh, old).astype(BF)

    st = jnp.where(step % (NH // SR) == 0, jnp.zeros((8, D), F32), st_ref[...])
    for p in range(SR // 2):
        b0 = step * SR + 2 * p
        lp0, lp1 = pos_ref[b0], pos_ref[b0 + 1]
        for r, b, lp in ((2 * p, b0, lp0), (2 * p + 1, b0 + 1, lp1)):
            ko_ref[r] = k_ref[r]
            vo_ref[r] = v_ref[r]
            patch(kn, ko_ref, r, b, lp)
            patch(vn, vo_ref, r, b, lp)
        q16 = qs[pl.ds(pl.multiple_of(b0 * 8, 16), 16), :]
        lhs = jnp.concatenate([q16[:8], q16[8:]], axis=1).astype(BF)
        keys = jnp.concatenate([ko_ref[2 * p], ko_ref[2 * p + 1]], axis=1)
        vals = jnp.concatenate([vo_ref[2 * p], vo_ref[2 * p + 1]], axis=1)
        valid = head_ok & (tok <= jnp.where(row < HL, lp0, lp1))
        m, l, o = pair_attend(lhs, keys, vals, valid, scale)
        o_ref[pl.ds(8 * p, 8), :] = o
        pair = (step % (NH // SR)) * (SR // 2) + p
        st = jnp.where(lane == pair, m, jnp.where(lane == pair + NQ, l, st))
    st_ref[...] = st


def self_attention(hidden, local_pos, k_self, v_self, g1, wq, wk, wv, cos, sin):
    T2 = k_self.shape[1]
    const = lambda i, p: (0, 0)
    blk = pl.BlockSpec((SR, T2, D), lambda i, p: (i, 0, 0))
    full = lambda a: pl.BlockSpec(a.shape, const)
    small = [hidden, g1, wq, wk, wv, cos, sin]
    return pl.pallas_call(
        self_kernel,
        grid_spec=pltpu.PrefetchScalarGridSpec(
            num_scalar_prefetch=1,
            grid=(NB // SR,),
            in_specs=[full(a) for a in small] + [blk, blk],
            out_specs=[blk, blk, pl.BlockSpec((SR * HL, D), lambda i, p: (i, 0)),
                       pl.BlockSpec((8, D), lambda i, p: (i // (NH // SR), 0))],
            scratch_shapes=[pltpu.VMEM((NB * 8, D), F32), pltpu.VMEM((NB * KL, D), F32), pltpu.VMEM((NB * KL, D), F32)],
        ),
        out_shape=[jax.ShapeDtypeStruct(k_self.shape, BF), jax.ShapeDtypeStruct(v_self.shape, BF),
                   jax.ShapeDtypeStruct((NB * HL, D), F32), jax.ShapeDtypeStruct((16, D), F32)],
        compiler_params=pltpu.CompilerParams(vmem_limit_bytes=VMEM_MAX),
        name="self_attn",
    )(local_pos, *small, k_self, v_self)


def peers():
    sp, tp = lax.axis_index("sp"), lax.axis_index("tp")
    core = lax.rem(tp, 2)
    return dict(sp=sp, core=core, y={"sp": 1 - sp}, c={"tp": tp + 1 - 2 * core}, x={"tp": lax.rem(tp + 2, 4)})


def entry_barrier(pe):
    barrier = pltpu.get_barrier_semaphore()
    for name in ("y", "c", "x"):
        pl.semaphore_signal(barrier, inc=1, device_id=pe[name], device_id_type=MESH)
    pl.semaphore_wait(barrier, 3)


def rcopy(src, dst, ssem, rsem, dev):
    return pltpu.make_async_remote_copy(src_ref=src, dst_ref=dst, send_sem=ssem, recv_sem=rsem,
                                        device_id=dev, device_id_type=MESH)


def tp_sum(pe, compute, finish, snd, rcv, chip, xr, sems):
    to_core = [rcopy(snd.at[j], rcv.at[j], sems.at[0, j], sems.at[1, j], pe["c"]) for j in range(NCH)]
    to_chip = [rcopy(chip.at[j], xr.at[j], sems.at[2, j], sems.at[3, j], pe["x"]) for j in range(NCH)]
    for j in range(NCH + 1):
        if j < NCH:
            part = compute(j)
            snd[j] = part[NQ:]
            chip[j] = part[:NQ]
            to_core[j].start()
        if j >= 1:
            to_core[j - 1].wait_recv()
            chip[j - 1] = chip[j - 1] + rcv[j - 1]
            to_chip[j - 1].start()
    for j in range(NCH):
        to_chip[j].wait_recv()
        finish(j, chip[j] + xr[j])
    for j in range(NCH):
        to_core[j].wait_send()
        to_chip[j].wait_send()


def share_rows(pe, own, x_ref, snd, rcv, sem):
    snd[...] = own.astype(F32)
    cp = rcopy(snd, rcv, sem.at[0], sem.at[1], pe["c"])
    cp.start()
    x_ref[pl.ds(0, NQ), :] = own
    cp.wait()
    x_ref[pl.ds(NQ, NQ), :] = rcv[...].astype(BF)


def mlp_act(x_ref, wg, wu, act, n_cols):
    step = 512
    for c in range(n_cols // step):
        s = slice(c * step, (c + 1) * step)
        gate = dot(x_ref[...], wg[:, s]).astype(BF).astype(F32)
        up = dot(x_ref[...], wu[:, s]).astype(BF).astype(F32)
        act[:, s] = (gate * jax.nn.sigmoid(gate) * up).astype(BF)


def cols(j):
    return slice(j * W, (j + 1) * W)


def heads_to_lanes(ref, core):
    parts = []
    for start in (core * NQ, (1 - core) * NQ):
        parts.append(jnp.concatenate([ref[pl.ds(start * HL + h, NQ, stride=HL), :] for h in range(HL)], axis=1))
    return jnp.concatenate(parts, axis=0).astype(BF)


SUM_SCRATCH = [pltpu.VMEM((NCH, NQ, W), F32)] * 4 + [pltpu.SemaphoreType.DMA((4, NCH))]
SHARE_SCRATCH = [pltpu.VMEM((NQ, HID), F32)] * 2 + [pltpu.SemaphoreType.DMA((2,))]


def mid_kernel(o_hbm, st_ref, hid_hbm, g2_ref, g3_ref, qn_ref, wo_hbm, wg_hbm, wu_hbm, wd_hbm, wq_hbm,
               qx_ref, h2_ref,
               wo, wg, wu, wd, wq, wsem, osnd, orcv, sts, str_, ysem, hown, att, xbuf, act, hres,
               a0, a1, a2, a3, asem, b0, b1, b2, b3, bsem, s0, s1, ssem, t0, t1, tsem):
    pe = peers()
    sp, core = pe["sp"], pe["core"]
    half = NH * HL
    local = [pltpu.make_async_copy(o_hbm.at[pl.ds(pl.multiple_of(sp * half, half), half)], att, wsem.at[5]),
             pltpu.make_async_copy(o_hbm.at[pl.ds(pl.multiple_of((1 - sp) * half, half), half)], osnd, wsem.at[6]),
             pltpu.make_async_copy(hid_hbm.at[pl.ds(pl.multiple_of(sp * NH + core * NQ, NQ), NQ)], hown, wsem.at[7])]
    for cp in local:
        cp.start()
    loads = [pltpu.make_async_copy(a, b, wsem.at[n])
             for n, (a, b) in enumerate(((wo_hbm, wo), (wg_hbm, wg), (wu_hbm, wu), (wd_hbm, wd), (wq_hbm, wq)))]
    for cp in loads:
        cp.start()
    entry_barrier(pe)
    both = st_ref[...]
    mine = jnp.where(sp == 0, both[:8], both[8:])
    sts[...] = jnp.where(sp == 0, both[8:], both[:8])
    local[1].wait()
    cp_o = rcopy(osnd, orcv, ysem.at[0], ysem.at[1], pe["y"])
    cp_s = rcopy(sts, str_, ysem.at[2], ysem.at[3], pe["y"])
    cp_s.start()
    cp_o.start()
    local[0].wait()
    local[2].wait()
    cp_s.wait()
    theirs = str_[...]
    top = jnp.maximum(mine, theirs)
    f1, f2 = jnp.exp(mine - top), jnp.exp(theirs - top)
    den = pltpu.roll(mine, NQ, 1) * f1 + pltpu.roll(theirs, NQ, 1) * f2
    c1, c2 = f1 / den, f2 / den
    cp_o.wait()
    for p in range(NQ):
        s = pl.ds(8 * p, 8)
        att[s, :] = att[s, :] * c1[:, p:p + 1] + orcv[s, :] * c2[:, p:p + 1]
    lhs = heads_to_lanes(att, core)

    loads[0].wait()

    def done1(j, total):
        hres[:, cols(j)] = (hown[:, cols(j)].astype(F32) + total).astype(BF)

    tp_sum(pe, lambda j: dot(lhs, wo[:, cols(j)]), done1, a0, a1, a2, a3, asem)
    share_rows(pe, norm32(hres[...].astype(F32), g2_ref[...].astype(F32)), xbuf, s0, s1, ssem)
    loads[1].wait()
    loads[2].wait()
    mlp_act(xbuf, wg, wu, act, act.shape[1])
    loads[3].wait()

    def done2(j, total):
        h2_ref[:, cols(j)] = (hres[:, cols(j)].astype(F32) + total).astype(BF)

    tp_sum(pe, lambda j: dot(act[...], wd[:, cols(j)]), done2, b0, b1, b2, b3, bsem)
    share_rows(pe, norm32(h2_ref[...].astype(F32), g3_ref[...].astype(F32)), xbuf, t0, t1, tsem)
    loads[4].wait()
    q = dot(xbuf[...], wq[...])
    gain = qn_ref[...].astype(F32)
    heads = [norm32(q[:, h * D:(h + 1) * D].astype(BF).astype(F32), gain).astype(F32) for h in range(HL)]
    spread_heads(qx_ref, [h[:NQ] for h in heads], core * NQ, NQ)
    spread_heads(qx_ref, [h[NQ:] for h in heads], (1 - core) * NQ, NQ)


def mid_stage(o, st, hidden, g2, g3, qn, wo, wg, wu, wd, wq):
    F = wg.shape[1]
    return pl.pallas_call(
        mid_kernel,
        in_specs=[ANY, VM, ANY, VM, VM, VM] + [ANY] * 5,
        out_specs=[VM, VM],
        out_shape=[jax.ShapeDtypeStruct((NH * 8, D), F32), jax.ShapeDtypeStruct((NQ, HID), BF)],
        scratch_shapes=[pltpu.VMEM(wo.shape, BF), pltpu.VMEM(wg.shape, BF), pltpu.VMEM(wu.shape, BF),
                        pltpu.VMEM(wd.shape, BF), pltpu.VMEM(wq.shape, BF), pltpu.SemaphoreType.DMA((8,)),
                        pltpu.VMEM((NH * HL, D), F32), pltpu.VMEM((NH * HL, D), F32),
                        pltpu.VMEM((8, D), F32), pltpu.VMEM((8, D), F32), pltpu.SemaphoreType.DMA((4,)),
                        pltpu.VMEM((NQ, HID), BF), pltpu.VMEM((NH * HL, D), F32), pltpu.VMEM((NH, HID), BF),
                        pltpu.VMEM((NH, F), BF), pltpu.VMEM((NQ, HID), BF)]
        + SUM_SCRATCH + SUM_SCRATCH + SHARE_SCRATCH + SHARE_SCRATCH,
        compiler_params=pltpu.CompilerParams(collective_id=0, has_side_effects=True, vmem_limit_bytes=VMEM_MAX),
        name="mid_stage",
    )(o, st, hidden, g2, g3, qn, wo, wg, wu, wd, wq)


CR = 8


def cross_kernel(meta_ref, q_ref, k_ref, v_ref, o_ref):
    step = pl.program_id(0)
    T2 = k_ref.shape[1]
    scale = D ** -0.5
    col = lax.broadcasted_iota(jnp.int32, (8, T2), 1)
    row = lax.broadcasted_iota(jnp.int32, (8, T2), 0)
    tok = col // KL
    head_ok = (col % KL) == ((row % HL) // (HL // KL))
    for p in range(CR // 2):
        b0 = meta_ref[0] * NH + step * CR + 2 * p
        n0, n1 = meta_ref[1 + b0], meta_ref[2 + b0]
        q16 = q_ref[pl.ds(16 * p, 16), :]
        lhs = jnp.concatenate([q16[:8], q16[8:]], axis=1).astype(BF)
        keys = jnp.concatenate([k_ref[2 * p], k_ref[2 * p + 1]], axis=1)
        vals = jnp.concatenate([v_ref[2 * p], v_ref[2 * p + 1]], axis=1)
        valid = head_ok & (tok < jnp.where(row < HL, n0, n1))
        m, l, o = pair_attend(lhs, keys, vals, valid, scale)
        o_ref[pl.ds(8 * p, 8), :] = o / l


def cross_attention(q, meta, k_cross, v_cross):
    T2 = k_cross.shape[1]
    blk = pl.BlockSpec((CR, T2, D), lambda i, m: (m[0] * (NH // CR) + i, 0, 0))
    return pl.pallas_call(
        cross_kernel,
        grid_spec=pltpu.PrefetchScalarGridSpec(
            num_scalar_prefetch=1,
            grid=(NH // CR,),
            in_specs=[pl.BlockSpec((CR * 8, D), lambda i, m: (i, 0)), blk, blk],
            out_specs=pl.BlockSpec((CR * HL, D), lambda i, m: (i, 0)),
        ),
        out_shape=jax.ShapeDtypeStruct((NH * HL, D), F32),
        compiler_params=pltpu.CompilerParams(vmem_limit_bytes=VMEM_MAX),
        name="cross_attn",
    )(meta, q, k_cross, v_cross)


def last_kernel(att_ref, h2_ref, g4_ref, gates_ref, mask_ref, wo_hbm, wg_hbm, wu_hbm, wd_hbm,
                out_ref,
                wo, wg, wu, wd, wsem, xbuf, act, hres, fin, yr, cr, gsem,
                a0, a1, a2, a3, asem, b0, b1, b2, b3, bsem, s0, s1, ssem):
    pe = peers()
    sp, core = pe["sp"], pe["core"]
    loads = [pltpu.make_async_copy(a, b, wsem.at[n])
             for n, (a, b) in enumerate(((wo_hbm, wo), (wg_hbm, wg), (wu_hbm, wu), (wd_hbm, wd)))]
    for cp in loads:
        cp.start()
    entry_barrier(pe)
    lhs = heads_to_lanes(att_ref, core)

    def rows(half, of_core):
        return pl.ds(pl.multiple_of(half * NH + of_core * NQ, NQ), NQ)

    row_scale = mask_ref[rows(sp, core), :]
    gates = jnp.tanh(gates_ref[...])
    gate0, gate1 = gates[:, 0:1] * row_scale, gates[:, 1:2] * row_scale
    loads[0].wait()

    def done3(j, total):
        hres[:, cols(j)] = (h2_ref[:, cols(j)].astype(F32) + gate0 * total).astype(BF)

    tp_sum(pe, lambda j: dot(lhs, wo[:, cols(j)]), done3, a0, a1, a2, a3, asem)
    share_rows(pe, norm32(hres[...].astype(F32), g4_ref[...].astype(F32)), xbuf, s0, s1, ssem)
    loads[1].wait()
    loads[2].wait()
    mlp_act(xbuf, wg, wu, act, act.shape[1])
    loads[3].wait()

    to_y = [rcopy(fin.at[j], yr.at[j], gsem.at[0, j], gsem.at[1, j], pe["y"]) for j in range(NCH)]
    to_c = [rcopy(fin.at[j], cr.at[0, j], gsem.at[2, j], gsem.at[3, j], pe["c"]) for j in range(NCH)]
    pass_c = [rcopy(yr.at[j], cr.at[1, j], gsem.at[4, j], gsem.at[5, j], pe["c"]) for j in range(NCH)]

    def done4(j, total):
        res = (hres[:, cols(j)].astype(F32) + gate1 * total).astype(BF)
        out_ref[rows(sp, core), cols(j)] = res
        fin[j] = res.astype(F32)
        to_y[j].start()
        to_c[j].start()
        if j >= 1:
            to_y[j - 1].wait_recv()
            pass_c[j - 1].start()

    tp_sum(pe, lambda j: dot(act[...], wd[:, cols(j)]), done4, b0, b1, b2, b3, bsem)
    to_y[NCH - 1].wait_recv()
    pass_c[NCH - 1].start()
    for j in range(NCH):
        out_ref[rows(1 - sp, core), cols(j)] = yr[j].astype(BF)
        to_c[j].wait_recv()
        out_ref[rows(sp, 1 - core), cols(j)] = cr[0, j].astype(BF)
    for j in range(NCH):
        pass_c[j].wait_recv()
        out_ref[rows(1 - sp, 1 - core), cols(j)] = cr[1, j].astype(BF)
    for j in range(NCH):
        to_y[j].wait_send()
        to_c[j].wait_send()
        pass_c[j].wait_send()


def last_stage(att, h2, g4, gates, mask, wo, wg, wu, wd):
    F = wg.shape[1]
    return pl.pallas_call(
        last_kernel,
        in_specs=[VM] * 5 + [ANY] * 4,
        out_specs=VM,
        out_shape=jax.ShapeDtypeStruct((NB, HID), BF),
        scratch_shapes=[pltpu.VMEM(wo.shape, BF), pltpu.VMEM(wg.shape, BF), pltpu.VMEM(wu.shape, BF),
                        pltpu.VMEM(wd.shape, BF), pltpu.SemaphoreType.DMA((4,)),
                        pltpu.VMEM((NH, HID), BF), pltpu.VMEM((NH, F), BF), pltpu.VMEM((NQ, HID), BF),
                        pltpu.VMEM((NCH, NQ, W), F32), pltpu.VMEM((NCH, NQ, W), F32),
                        pltpu.VMEM((2, NCH, NQ, W), F32), pltpu.SemaphoreType.DMA((6, NCH))]
        + SUM_SCRATCH + SUM_SCRATCH + SHARE_SCRATCH,
        compiler_params=pltpu.CompilerParams(collective_id=1, has_side_effects=True, vmem_limit_bytes=VMEM_MAX),
        name="last_stage",
    )(att, h2, g4, gates, mask, wo, wg, wu, wd)


def solution(mesh):
    cache_spec = P('dp', 'sp', 'tp', None)
    cross_spec = P('dp', None, 'tp', None)
    row_spec = P('dp', None)
    vec_spec = P('dp')
    full_spec = P(None)
    col_spec = P(None, 'tp')
    split_rows = P('tp', None)
    in_specs = (row_spec, vec_spec, cache_spec, cache_spec, cross_spec, cross_spec, row_spec, vec_spec,
                full_spec, col_spec, col_spec, col_spec, split_rows, full_spec, col_spec, col_spec, split_rows,
                full_spec, col_spec, full_spec, split_rows, full_spec, full_spec, col_spec, col_spec, split_rows)
    out_specs = (row_spec, cache_spec, cache_spec)

    def local_step(hidden, new_pos, k_self, v_self, k_cross, v_cross, xvalid, rowmask,
                   self_attn_norm, self_wq, self_wk, self_wv, self_wo, self_mlp_norm,
                   self_wgate, self_wup, self_wdown, cross_attn_norm, cross_wq, cross_qnorm,
                   cross_wo, cross_gates, cross_mlp_norm, cross_wgate, cross_wup, cross_wdown):
        sp = lax.axis_index('sp')
        len_local = k_self.shape[1]
        angles = new_pos.astype(F32)[:, None] * rope_freqs(D)[None, :]
        cos_t, sin_t = jnp.cos(angles), jnp.sin(angles)
        cos = jnp.concatenate([cos_t, cos_t], axis=1)
        sin = jnp.concatenate([-sin_t, sin_t], axis=1)
        flat = lambda a: a.reshape(a.shape[0], a.shape[1] * a.shape[2], a.shape[3])
        row = lambda a: a.reshape(1, -1)
        k_out, v_out, o, st = self_attention(
            hidden, new_pos - sp * len_local, flat(k_self), flat(v_self), row(self_attn_norm),
            self_wq, self_wk, self_wv, cos, sin)
        qx, h2 = mid_stage(o, st, hidden, row(self_mlp_norm), row(cross_attn_norm), row(cross_qnorm),
                           self_wo, self_wgate, self_wup, self_wdown, cross_wq)
        counts = jnp.sum((xvalid > 0).astype(jnp.int32), axis=1)
        meta = jnp.concatenate([sp.astype(jnp.int32)[None], counts])
        att = cross_attention(qx, meta, flat(k_cross), flat(v_cross))
        h4 = last_stage(att, h2, row(cross_mlp_norm), row(cross_gates.astype(F32)),
                        rowmask.astype(F32)[:, None], cross_wo, cross_wgate, cross_wup, cross_wdown)
        return h4, k_out.reshape(k_self.shape), v_out.reshape(v_self.shape)

    return jax.shard_map(local_step, mesh=mesh, in_specs=in_specs, out_specs=out_specs, check_vma=False)
```

time: 439 us -> 184 us (0.42); the launches traced: 431 us -> 184 us
  waiting for transfers between devices: 191 us -> 0 us
  Pallas kernels: 0 us -> 170 us
  matrix products: 121 us -> 0 us
  other arithmetic: 70 us -> 5.23 us
  blocking collectives: 28.1 us -> 0 us
  between operations: 14.5 us -> 0.67 us
    psum x5 -> x0, waiting for transfers between devices: 191 us -> none  [the longest x1 45.9 us: local_step(): lax.psum(mlp_partial(rms_norm(after_cross, cross_mlp_norm), cross_wgate,...]
    pallas_call x0 -> x4, Pallas kernels: none -> 170 us  [the longest x1 48.1 us: mid_stage(): pl.pallas_call(mid_kernel, in_specs=[ANY, VM, ANY, VM, VM, VM] + [ANY] *...]
    dot_general x14 -> x0, matrix products: 121 us -> none  [the longest x2 39.2 us: local_softmax(): jnp.einsum('bkgd,btkd->bkgt', queries, key_rows, preferred_element_type=j...]
    select_n x1 -> x0, other arithmetic: 46 us -> none  [local_step(): k_new_cache = jnp.where(hit_mask, key_new[:, None], k_self)]
    psum x1 -> x0, blocking collectives: 14.7 us -> none  [combine_sp(): total_sum = lax.psum(part_sum * factor, 'sp')]
    pmax x1 -> x0, blocking collectives: 13.4 us -> none  [combine_sp(): glob_max = lax.pmax(part_max, 'sp')]
    reduce_sum x6 -> x1, other arithmetic: 9.51 us -> 1.17 us  [local_step(): counts = jnp.sum((xvalid > 0).astype(jnp.int32), axis=1)]
    reshape x2 -> x4, local copies, waits for them, and re-layouts: 0.21 us -> 5.14 us  [local_step(): row = lambda a: a.reshape(1, -1)]
  transfers between devices with their start and end apart: 5 -> 0, of which waited for: 5 -> 0; matrix products, arithmetic and copies ran while one was open for 0% -> 0% of each run, Pallas kernels for 0% -> 0%
where the time goes in v1:
time: 184 us
  Pallas kernels  170 us (92%)
  local copies, waits for them, and re-layouts  8.25 us (4%)
  other arithmetic  5.23 us (3%)
    pallas_call x1, Pallas kernels, mid_stage(): pl.pallas_call(mid_kernel, in_specs=[ANY, VM, ANY, VM, VM, VM] + [ANY] *...  48.1 us
    pallas_call x1, Pallas kernels, self_attention(): pl.pallas_call(self_kernel, grid_spec=pltpu.PrefetchScalarGridSpec(num_sc...  43.4 us
    pallas_call x1, Pallas kernels, last_stage(): pl.pallas_call(last_kernel, in_specs=[VM] * 5 + [ANY] * 4, out_specs=VM,...  42.5 us
    pallas_call x1, Pallas kernels, cross_attention(): pl.pallas_call(cross_kernel, grid_spec=pltpu.PrefetchScalarGridSpec(num_s...  35.7 us
    reshape x4, local copies, waits for them, and re-layouts, local_step(): row = lambda a: a.reshape(1, -1)  5.14 us

profile of v1, /device:TPU:0, one launch (start us, length us, event | category | flops | bytes accessed | tf_op | source)
XLA Modules:
  0.0 183.7 jit_solution(6309892344269083553)
XLA Ops:
  0.7 1.2 convert_reduce_fusion
  1.8 0.7 pad_add_fusion.meta_ref
  2.5 0.7 convert_element_type.19
  3.2 1.3 fusion.1
  4.5 1.3 reshape.67.g_ref
  5.8 1.3 reshape.70.g2_ref
  7.1 1.3 reshape.71.g3_ref
  8.4 1.3 reshape.75.g4_ref
  9.6 0.8 copy.29.mask_ref
  10.5 0.5 fusion
  11.0 0.8 pad_maximum_fusion
  11.8 43.4 %self_attn.1 = (bf16[256,256,128]{2,1,0:T(8,128)(2,1)}, bf16[256,256,128]{2,1,0:T(8,128)(2,1)}, f32[1024,128]{1,0:T(8,128)}, f32[16,128]{1,0:T(8,128)}) custom-call(s32[256]{0:T(256)} %get-tuple-element.19.pos_ref, bf16[256,2048]{1,0:T(8,128)(2,1)} %hid_hbm.1, bf16[1,2048]{1,0:T(2,128)(2,1)} %reshape.67.g_ref, bf16[2048,512]{1,0:T(8,128)(2,1)} %wq_ref.1, ...), custom_call_target="tpu_custom_call" | custom-call | tf_op jit(solution)/shard_map/self_attn/pallas_call | solution.py:141
  55.2 48.1 %mid_stage.1 = (f32[1024,128]{1,0:T(8,128)}, bf16[64,2048]{1,0:T(8,128)(2,1)}) custom-call(f32[1024,128]{1,0:T(8,128)} %get-tuple-element.9.o_hbm, f32[16,128]{1,0:T(8,128)} %get-tuple-element.10.st_ref, bf16[256,2048]{1,0:T(8,128)(2,1)} %hid_hbm.1, bf16[1,2048]{1,0:T(2,128)(2,1)} %reshape.70.g2_ref, bf16[1,2048]{1,0:T(2,128)(2,1)} %reshape.71.g3_ref, ...), custom_call_target="tpu_custom_call" | custom-call | tf_op jit(solution)/shard_map/mid_stage/pallas_call | solution.py:296
  103.3 35.7 %cross_attn.1.att_ref = f32[512,128]{1,0:T(8,128)} custom-call(s32[257]{0:T(512)} %pad_add_fusion.meta_ref, f32[1024,128]{1,0:T(8,128)} %get-tuple-element.11.q_ref, bf16[256,1024,128]{2,1,0:T(8,128)(2,1)} %bitcast.4.k_ref, bf16[256,1024,128]{2,1,0:T(8,128)(2,1)} %bitcast.5.v_ref), custom_call_target="tpu_custom_call" | custom-call | tf_op jit(solution)/shard_map/cross_attn/pallas_call | solution.py:339
  139.0 42.5 %last_stage.1 = bf16[256,2048]{1,0:T(8,128)(2,1)} custom-call(f32[512,128]{1,0:T(8,128)} %cross_attn.1.att_ref, bf16[64,2048]{1,0:T(8,128)(2,1)} %get-tuple-element.12.h2_ref, bf16[1,2048]{1,0:T(2,128)(2,1)} %reshape.75.g4_ref, f32[1,2]{1,0:T(1,128)} %bitcast.14, f32[256,1]{1,0:T(8,128)} %copy.29.mask_ref, bf16[512,2048]{1,0:T(8,128)(2,1)} %wo_hbm.3, ...), custom_call_target="tpu_custom_call" | custom-call | tf_op jit(solution)/shard_map/last_stage/pallas_call | solution.py:416
  181.4 2.3 %copy.31 = bf16[256,2048]{1,0:T(8,128)(2,1)} copy(bf16[256,2048]{1,0:T(8,128)(2,1)} %last_stage.1) | data formatting | bytes 2097152
  (1 shorter events, 0.0 us)

commit v2 on v1

v2 whole, which is shorter than its diff:
```python
import functools
import math
import numpy as np
import jax
import jax.numpy as jnp
from jax import lax
from jax.experimental import pallas as pl
from jax.experimental.pallas import tpu as pltpu
from jax.sharding import PartitionSpec as P

NORM_EPS = 1e-5
ROPE_THETA = 500000.0
ROPE_FACTOR = 8.0
LOW_FREQ = 1.0
HIGH_FREQ = 4.0
ORIG_CTX = 8192.0
NEG_BIG = -1e30

BF = jnp.bfloat16
F32 = jnp.float32
D = 128
HL = 4
KL = 2
NB = 256
NH = 128
NQ = 64
HID = 2048
NCH = 4
W = HID // NCH
VMEM_MAX = 66 * 1024 * 1024 - 2 * 1024 * 1024
MESH = pl.DeviceIdType.MESH
ANY = pl.BlockSpec(memory_space=pl.ANY)
VM = pl.BlockSpec(memory_space=pltpu.VMEM)


def rope_freqs(head_dim):
    inv_freq = 1.0 / (ROPE_THETA ** (np.arange(0, head_dim, 2) / head_dim))
    wavelen = 2.0 * math.pi / inv_freq
    smooth = (ORIG_CTX / wavelen - LOW_FREQ) / (HIGH_FREQ - LOW_FREQ)
    mid_freq = (1.0 - smooth) * inv_freq / ROPE_FACTOR + smooth * inv_freq
    scaled = np.where(wavelen > ORIG_CTX / LOW_FREQ, inv_freq / ROPE_FACTOR, mid_freq)
    scaled = np.where(wavelen < ORIG_CTX / HIGH_FREQ, inv_freq, scaled)
    return np.concatenate([scaled, scaled]).astype(np.float32)[None, :]


def norm32(vals32, gain32):
    inv = lax.rsqrt(jnp.mean(vals32 * vals32, axis=-1, keepdims=True) + NORM_EPS)
    return (vals32 * inv * gain32).astype(BF)


def dot(a, b):
    return jnp.dot(a, b, preferred_element_type=F32)


def dot_nt(a, b):
    return lax.dot_general(a, b, (((1,), (1,)), ((), ())), preferred_element_type=F32)


def attend(lhs, keys, vals, valid):
    first = lax.broadcasted_iota(jnp.int32, (8, D), 0) < HL
    s = [dot_nt(a, k) * (D ** -0.5) for a, k in zip(lhs, keys)]
    s = [jnp.where(ok, x, NEG_BIG) for ok, x in zip(valid, s)]
    m = [jnp.max(x, axis=-1, keepdims=True) for x in s]
    p = [jnp.where(ok, jnp.exp(x - t), 0.0) for ok, x, t in zip(valid, s, m)]
    l = [jnp.sum(x, axis=-1, keepdims=True) for x in p]
    o = [dot(x.astype(BF), v) for x, v in zip(p, vals)]
    return m, l, [jnp.where(first, x[:, :D], x[:, D:]) for x in o]


def pair_lhs(q_ref, b0):
    q16 = q_ref[pl.ds(pl.multiple_of(b0 * 8, 16), 16), :]
    return jnp.concatenate([q16[:8], q16[8:]], axis=1).astype(BF)


def column(vec, first, rows):
    n = vec.shape[1]
    at = lax.broadcasted_iota(jnp.int32, (rows, n), 1) == lax.broadcasted_iota(jnp.int32, (rows, n), 0) + first
    return jnp.sum(jnp.where(at, vec, 0.0), axis=1, keepdims=True)


def spread_heads(ref, heads, start, rows):
    odd = (lax.broadcasted_iota(jnp.int32, (rows, D), 0) % 2) == 1
    for h in range(HL):
        ref[pl.ds(start * 8 + h, rows, stride=8), :] = jnp.where(odd, 0.0, heads[h])
        ref[pl.ds(start * 8 + HL + h, rows, stride=8), :] = jnp.where(odd, heads[h], 0.0)


SR = 16
NS = 8
PRE = 5


def self_kernel(pos_ref, posv_ref, freq_ref, g_ref, hid_hbm, wq_hbm, wk_hbm, wv_hbm, k_hbm, v_hbm,
                ko_hbm, vo_hbm, o_ref, st_ref,
                hid, wq, wk, wv, wsem, kbuf, vbuf, isem, osem, qs, kn, vn):
    T2 = k_hbm.shape[1]
    steps = NB // SR
    first_pos = lax.axis_index("sp") * (T2 // KL)
    loads = [pltpu.make_async_copy(a, b, wsem.at[n])
             for n, (a, b) in enumerate(((hid_hbm, hid), (wq_hbm, wq), (wk_hbm, wk), (wv_hbm, wv)))]
    for cp in loads:
        cp.start()

    def into(i):
        rows, slot = pl.ds(pl.multiple_of(i * SR, SR), SR), i % NS
        return (pltpu.make_async_copy(k_hbm.at[rows], kbuf.at[slot], isem.at[0, slot]),
                pltpu.make_async_copy(v_hbm.at[rows], vbuf.at[slot], isem.at[1, slot]))

    def out_of(i):
        rows, slot = pl.ds(pl.multiple_of(i * SR, SR), SR), i % NS
        return (pltpu.make_async_copy(kbuf.at[slot], ko_hbm.at[rows], osem.at[0, slot]),
                pltpu.make_async_copy(vbuf.at[slot], vo_hbm.at[rows], osem.at[1, slot]))

    for i in range(PRE):
        for cp in into(i):
            cp.start()

    angle = column(posv_ref[...].astype(F32).reshape(1, NB), 0, NB) * freq_ref[...]
    cos, sin = jnp.cos(angle), jnp.sin(angle)
    sin = jnp.where(lax.broadcasted_iota(jnp.int32, (NB, D), 1) < D // 2, -sin, sin)

    def rope(part):
        part = part.astype(BF).astype(F32)
        return (part * cos + pltpu.roll(part, D // 2, 1) * sin).astype(BF).astype(F32)

    loads[0].wait()
    x = norm32(hid[...].astype(F32), g_ref[...].astype(F32).reshape(1, HID))
    loads[1].wait()
    q = dot(x, wq[...])
    spread_heads(qs, [rope(q[:, h * D:(h + 1) * D]) for h in range(HL)], 0, NB)
    loads[2].wait()
    k = dot(x, wk[...])
    loads[3].wait()
    v = dot(x, wv[...])
    for h in range(KL):
        kn[pl.ds(h, NB, stride=KL), :] = rope(k[:, h * D:(h + 1) * D])
        vn[pl.ds(h, NB, stride=KL), :] = v[:, h * D:(h + 1) * D].astype(BF).astype(F32)
    st_ref[...] = jnp.zeros_like(st_ref)

    col = lax.broadcasted_iota(jnp.int32, (8, T2), 1)
    row = lax.broadcasted_iota(jnp.int32, (8, T2), 0)
    tok = col // KL
    head_ok = (col % KL) == ((row % HL) // (HL // KL))
    lane = lax.broadcasted_iota(jnp.int32, (8, D), 1)
    i16 = lax.broadcasted_iota(jnp.int32, (16, D), 0)

    def patch(new_ref, dst_ref, slot, r, b, lp):
        base = pl.multiple_of((jnp.clip(lp, 0, T2 // KL - 1) // 8) * 16, 16)
        fresh = jnp.where(i16 % 2 == 0, new_ref[pl.ds(2 * b, 1), :], new_ref[pl.ds(2 * b + 1, 1), :])
        old = dst_ref[slot, r, pl.ds(base, 16), :].astype(F32)
        dst_ref[slot, r, pl.ds(base, 16), :] = jnp.where(base + i16 - i16 % 2 == 2 * lp, fresh, old).astype(BF)

    def body(i, _):
        slot = i % NS

        @pl.when(i >= NS - PRE)
        def _():
            for cp in out_of(i - (NS - PRE)):
                cp.wait()

        @pl.when(i + PRE < steps)
        def _():
            for cp in into(i + PRE):
                cp.start()

        for cp in into(i):
            cp.wait()
        lps = [pos_ref[i * SR + r] - first_pos for r in range(SR)]
        for r in range(SR):
            patch(kn, kbuf, slot, r, i * SR + r, lps[r])
            patch(vn, vbuf, slot, r, i * SR + r, lps[r])
        pairs = range(SR // 2)
        both = lambda buf, p: jnp.concatenate([buf[slot, 2 * p], buf[slot, 2 * p + 1]], axis=1)
        m, l, o = attend([pair_lhs(qs, i * SR + 2 * p) for p in pairs], [both(kbuf, p) for p in pairs],
                         [both(vbuf, p) for p in pairs],
                         [head_ok & (tok <= jnp.where(row < HL, lps[2 * p], lps[2 * p + 1])) for p in pairs])
        half = i // (NH // SR)
        srow = pl.ds(pl.multiple_of(half * 8, 8), 8)
        st = st_ref[srow, :]
        for p in pairs:
            o_ref[pl.ds(pl.multiple_of(i * SR * HL + 8 * p, 8), 8), :] = o[p]
            at = (i - half * (NH // SR)) * (SR // 2) + p
            st = jnp.where(lane == at, m[p], jnp.where(lane == at + NQ, l[p], st))
        st_ref[srow, :] = st
        for cp in out_of(i):
            cp.start()
        return 0

    lax.fori_loop(0, steps, body, 0)
    for i in range(steps - (NS - PRE), steps):
        for cp in out_of(i):
            cp.wait()


def self_attention(new_pos, g1, hidden, wq, wk, wv, k_self, v_self):
    T2 = k_self.shape[1]
    return pl.pallas_call(
        self_kernel,
        in_specs=[pl.BlockSpec(memory_space=pltpu.SMEM), VM, VM, VM] + [ANY] * 6,
        out_specs=[ANY, ANY, VM, VM],
        scratch_shapes=[pltpu.VMEM(hidden.shape, BF), pltpu.VMEM(wq.shape, BF), pltpu.VMEM(wk.shape, BF),
                        pltpu.VMEM(wv.shape, BF), pltpu.SemaphoreType.DMA((4,)),
                        pltpu.VMEM((NS, SR, T2, D), BF), pltpu.VMEM((NS, SR, T2, D), BF),
                        pltpu.SemaphoreType.DMA((2, NS)), pltpu.SemaphoreType.DMA((2, NS)),
                        pltpu.VMEM((NB * 8, D), F32), pltpu.VMEM((NB * KL, D), F32), pltpu.VMEM((NB * KL, D), F32)],
        out_shape=[jax.ShapeDtypeStruct(k_self.shape, BF), jax.ShapeDtypeStruct(v_self.shape, BF),
                   jax.ShapeDtypeStruct((NB * HL, D), F32), jax.ShapeDtypeStruct((16, D), F32)],
        compiler_params=pltpu.CompilerParams(vmem_limit_bytes=VMEM_MAX),
        name="self_attn",
    )(new_pos, new_pos, jnp.asarray(rope_freqs(D)), g1, hidden, wq, wk, wv, k_self, v_self)


def peers():
    sp, tp = lax.axis_index("sp"), lax.axis_index("tp")
    core = lax.rem(tp, 2)
    return dict(sp=sp, core=core, y={"sp": 1 - sp}, c={"tp": tp + 1 - 2 * core}, x={"tp": lax.rem(tp + 2, 4)})


def entry_barrier(pe):
    barrier = pltpu.get_barrier_semaphore()
    for name in ("y", "c", "x"):
        pl.semaphore_signal(barrier, inc=1, device_id=pe[name], device_id_type=MESH)
    pl.semaphore_wait(barrier, 3)


def rcopy(src, dst, ssem, rsem, dev):
    return pltpu.make_async_remote_copy(src_ref=src, dst_ref=dst, send_sem=ssem, recv_sem=rsem,
                                        device_id=dev, device_id_type=MESH)


def tp_sum(pe, compute, finish, snd, rcv, chip, xr, sems):
    to_core = [rcopy(snd.at[j], rcv.at[j], sems.at[0, j], sems.at[1, j], pe["c"]) for j in range(NCH)]
    to_chip = [rcopy(chip.at[j], xr.at[j], sems.at[2, j], sems.at[3, j], pe["x"]) for j in range(NCH)]
    for j in range(NCH + 1):
        if j < NCH:
            part = compute(j)
            snd[j] = part[NQ:]
            chip[j] = part[:NQ]
            to_core[j].start()
        if j >= 1:
            to_core[j - 1].wait_recv()
            chip[j - 1] = chip[j - 1] + rcv[j - 1]
            to_chip[j - 1].start()
    for j in range(NCH):
        to_chip[j].wait_recv()
        finish(j, chip[j] + xr[j])
    for j in range(NCH):
        to_core[j].wait_send()
        to_chip[j].wait_send()


def share_rows(pe, own, x_ref, snd, rcv, sem):
    snd[...] = own.astype(F32)
    cp = rcopy(snd, rcv, sem.at[0], sem.at[1], pe["c"])
    cp.start()
    x_ref[pl.ds(0, NQ), :] = own
    cp.wait()
    x_ref[pl.ds(NQ, NQ), :] = rcv[...].astype(BF)


def mlp_act(x_ref, wg, wu, act, n_cols):
    step = 512
    for c in range(n_cols // step):
        s = slice(c * step, (c + 1) * step)
        gate = dot(x_ref[...], wg[:, s]).astype(BF).astype(F32)
        up = dot(x_ref[...], wu[:, s]).astype(BF).astype(F32)
        act[:, s] = (gate * jax.nn.sigmoid(gate) * up).astype(BF)


def cols(j):
    return slice(j * W, (j + 1) * W)


def heads_to_lanes(ref, starts, rows):
    parts = [jnp.concatenate([ref[pl.ds(s * HL + h, rows, stride=HL), :] for h in range(HL)], axis=1) for s in starts]
    return jnp.concatenate(parts, axis=0).astype(BF)


CR = 8
NR = 5
RC = NQ // NCH
XB = 2 * RC // CR


def rest_kernel(o_hbm, st_ref, hid_hbm, g2_ref, g3_ref, qn_ref, g4_ref, gates_ref, mask_ref, valid_hbm,
                wo_hbm, wg_hbm, wu_hbm, wd_hbm, wq_hbm, wo2_hbm, wg2_hbm, wu2_hbm, wd2_hbm, k_hbm, v_hbm,
                out_ref,
                wo, wg, wu, wd, wq, wo2, wsem, kbuf, vbuf, ksem, osnd, orcv, sts, str_, ysem, hown, att, valid, cnt,
                qx, xbuf, act, hres, h2, fin, yr, cr, gsem,
                a0, a1, a2, a3, asem, b0, b1, b2, b3, bsem, c0, c1, c2, c3, csem, dsem,
                s0, s1, ssem, t0, t1, tsem, esem):
    pe = peers()
    sp, core = pe["sp"], pe["core"]
    T2 = k_hbm.shape[1]
    half = NH * HL
    blocks = NH // CR

    local = [pltpu.make_async_copy(o_hbm.at[pl.ds(pl.multiple_of((1 - sp) * half, half), half)], osnd, wsem.at[6]),
             pltpu.make_async_copy(o_hbm.at[pl.ds(pl.multiple_of(sp * half, half), half)], att, wsem.at[7]),
             pltpu.make_async_copy(hid_hbm.at[pl.ds(pl.multiple_of(sp * NH + core * NQ, NQ), NQ)], hown, wsem.at[8]),
             pltpu.make_async_copy(valid_hbm.at[pl.ds(pl.multiple_of(sp * NH, NH), NH)], valid, wsem.at[9])]
    pairs = ((wo_hbm, wo), (wg_hbm, wg), (wu_hbm, wu), (wd_hbm, wd), (wq_hbm, wq), (wo2_hbm, wo2))
    loads = [pltpu.make_async_copy(a, b, wsem.at[n]) for n, (a, b) in enumerate(pairs)]
    for cp in local + loads:
        cp.start()

    def block_row(t):
        chunk, of_core, sub = t // XB, (t % XB) // (XB // 2), t % (XB // 2)
        return of_core * NQ + chunk * RC + sub * CR

    def kv_loads(t):
        rows, slot = pl.ds(pl.multiple_of(sp * NH + block_row(t), CR), CR), t % NR
        return (pltpu.make_async_copy(k_hbm.at[rows], kbuf.at[slot], ksem.at[0, slot]),
                pltpu.make_async_copy(v_hbm.at[rows], vbuf.at[slot], ksem.at[1, slot]))

    for t in range(NR):
        for cp in kv_loads(t):
            cp.start()

    entry_barrier(pe)
    both = st_ref[...]
    mine = jnp.where(sp == 0, both[:8], both[8:])
    sts[...] = jnp.where(sp == 0, both[8:], both[:8])
    local[0].wait()
    cp_o = rcopy(osnd, orcv, ysem.at[0], ysem.at[1], pe["y"])
    cp_s = rcopy(sts, str_, ysem.at[2], ysem.at[3], pe["y"])
    cp_s.start()
    cp_o.start()
    for cp in local[1:]:
        cp.wait()
    some = jnp.sum((valid[...] > 0).astype(jnp.int32), axis=1, keepdims=True)
    cnt[...] = jnp.broadcast_to(some, cnt.shape)
    row_scale = column(mask_ref[...].astype(F32).reshape(1, NB), sp * NH + core * NQ, NQ)
    gate0 = jnp.tanh(jnp.full((8, D), gates_ref[0], F32))[0:1, 0:1] * row_scale
    gate1 = jnp.tanh(jnp.full((8, D), gates_ref[1], F32))[0:1, 0:1] * row_scale
    cp_s.wait()
    theirs = str_[...]
    top = jnp.maximum(mine, theirs)
    f1, f2 = jnp.exp(mine - top), jnp.exp(theirs - top)
    den = pltpu.roll(mine, NQ, 1) * f1 + pltpu.roll(theirs, NQ, 1) * f2
    w1, w2 = f1 / den, f2 / den
    cp_o.wait()
    for p in range(NQ):
        s = pl.ds(8 * p, 8)
        att[s, :] = att[s, :] * w1[:, p:p + 1] + orcv[s, :] * w2[:, p:p + 1]
    lhs = heads_to_lanes(att, (core * NQ, (1 - core) * NQ), NQ)
    gain = lambda ref: ref[...].astype(F32).reshape(1, HID)

    loads[0].wait()

    def done1(j, total):
        hres[:, cols(j)] = (hown[:, cols(j)].astype(F32) + total).astype(BF)

    tp_sum(pe, lambda j: dot(lhs, wo[:, cols(j)]), done1, a0, a1, a2, a3, asem)
    share_rows(pe, norm32(hres[...].astype(F32), gain(g2_ref)), xbuf, s0, s1, ssem)
    loads[1].wait()
    loads[2].wait()
    mlp_act(xbuf, wg, wu, act, act.shape[1])
    loads[3].wait()

    def done2(j, total):
        if j == 0:
            for cp in loads2:
                cp.start()
        h2[:, cols(j)] = (hres[:, cols(j)].astype(F32) + total).astype(BF)

    loads2 = [pltpu.make_async_copy(a, b, wsem.at[1 + n])
              for n, (a, b) in enumerate(((wg2_hbm, wg), (wu2_hbm, wu), (wd2_hbm, wd)))]
    tp_sum(pe, lambda j: dot(act[...], wd[:, cols(j)]), done2, b0, b1, b2, b3, bsem)
    share_rows(pe, norm32(h2[...].astype(F32), gain(g3_ref)), xbuf, t0, t1, tsem)
    loads[4].wait()
    q = dot(xbuf[...], wq[...])
    qgain = qn_ref[...].astype(F32).reshape(1, D)
    heads = [norm32(q[:, h * D:(h + 1) * D].astype(BF).astype(F32), qgain).astype(F32) for h in range(HL)]
    spread_heads(qx, [h[:NQ] for h in heads], core * NQ, NQ)
    spread_heads(qx, [h[NQ:] for h in heads], (1 - core) * NQ, NQ)
    loads[5].wait()

    col = lax.broadcasted_iota(jnp.int32, (8, T2), 1)
    row = lax.broadcasted_iota(jnp.int32, (8, T2), 0)
    tok = col // KL
    head_ok = (col % KL) == ((row % HL) // (HL // KL))
    first = lax.broadcasted_iota(jnp.int32, (8, D), 0) < HL

    def block(t, _):
        slot = t % NR
        r0 = pl.multiple_of(block_row(t), CR)
        for cp in kv_loads(t):
            cp.wait()
        ps = range(CR // 2)
        lane_pair = lambda buf, p: jnp.concatenate([buf[slot, 2 * p], buf[slot, 2 * p + 1]], axis=1)
        n8 = cnt[pl.ds(r0, CR), :]
        limit = [jnp.concatenate([jnp.where(first, n8[2 * p:2 * p + 1], n8[2 * p + 1:2 * p + 2])] * (T2 // D), axis=1)
                 for p in ps]
        m, l, o = attend([pair_lhs(qx, r0 + 2 * p) for p in ps], [lane_pair(kbuf, p) for p in ps],
                         [lane_pair(vbuf, p) for p in ps], [head_ok & (tok < n) for n in limit])
        for p in ps:
            att[pl.ds(pl.multiple_of(r0 * HL + 8 * p, 8), 8), :] = o[p] / l[p]

        @pl.when(t + NR < blocks)
        def _():
            for cp in kv_loads(t + NR):
                cp.start()
        return 0

    to_core = [rcopy(c0.at[j], c1.at[j], csem.at[0, j], csem.at[1, j], pe["c"]) for j in range(NCH)]
    to_chip = [rcopy(c2.at[j], c3.at[j], csem.at[2, j], csem.at[3, j], pe["x"]) for j in range(NCH)]
    share = [rcopy(s0.at[pl.ds(j * RC, RC)], s1.at[pl.ds(j * RC, RC)], dsem.at[0, j], dsem.at[1, j], pe["c"])
             for j in range(NCH)]

    def pass_chip(j):
        to_core[j].wait_recv()
        c2[j] = c2[j] + c1[j]
        to_chip[j].start()

    def close(j):
        mine = slice(j * RC, (j + 1) * RC)
        to_chip[j].wait_recv()
        hres[mine, :] = (h2[mine, :].astype(F32) + gate0[mine] * (c2[j] + c3[j])).astype(BF)
        own = norm32(hres[mine, :].astype(F32), gain(g4_ref))
        s0[mine, :] = own.astype(F32)
        share[j].start()
        xbuf[mine, :] = own

    for j in range(NCH):
        lax.fori_loop(j * XB, j * XB + 1, block, 0)
        if j >= 1:
            pass_chip(j - 1)
        lax.fori_loop(j * XB + 1, (j + 1) * XB, block, 0)
        lhs = heads_to_lanes(att, (core * NQ + j * RC, (1 - core) * NQ + j * RC), RC)
        for n in range(NCH):
            part = dot(lhs, wo2[:, cols(n)])
            c0[j, :, cols(n)] = part[RC:]
            c2[j, :, cols(n)] = part[:RC]
        to_core[j].start()
        if j >= 1:
            close(j - 1)
    pass_chip(NCH - 1)
    close(NCH - 1)
    for j in range(NCH):
        share[j].wait_recv()
        xbuf[pl.ds(NQ + j * RC, RC), :] = s1[pl.ds(j * RC, RC), :].astype(BF)
    for j in range(NCH):
        to_core[j].wait_send()
        to_chip[j].wait_send()
        share[j].wait_send()
    for cp in loads2[:2]:
        cp.wait()
    mlp_act(xbuf, wg, wu, act, act.shape[1])
    loads2[2].wait()

    to_y = [rcopy(fin.at[j], yr.at[j], gsem.at[0, j], gsem.at[1, j], pe["y"]) for j in range(NCH)]
    to_c = [rcopy(fin.at[j], cr.at[0, j], gsem.at[2, j], gsem.at[3, j], pe["c"]) for j in range(NCH)]
    pass_c = [rcopy(yr.at[j], cr.at[1, j], gsem.at[4, j], gsem.at[5, j], pe["c"]) for j in range(NCH)]

    def rows(of_half, of_core):
        return pl.ds(pl.multiple_of(of_half * NH + of_core * NQ, NQ), NQ)

    def done4(j, total):
        res = (hres[:, cols(j)].astype(F32) + gate1 * total).astype(BF)
        out_ref[rows(sp, core), cols(j)] = res
        fin[j] = res.astype(F32)
        to_y[j].start()
        to_c[j].start()
        if j >= 1:
            to_y[j - 1].wait_recv()
            pass_c[j - 1].start()

    tp_sum(pe, lambda j: dot(act[...], wd[:, cols(j)]), done4, a0, a1, a2, a3, esem)
    to_y[NCH - 1].wait_recv()
    pass_c[NCH - 1].start()
    for j in range(NCH):
        out_ref[rows(1 - sp, core), cols(j)] = yr[j].astype(BF)
        to_c[j].wait_recv()
        out_ref[rows(sp, 1 - core), cols(j)] = cr[0, j].astype(BF)
    for j in range(NCH):
        pass_c[j].wait_recv()
        out_ref[rows(1 - sp, 1 - core), cols(j)] = cr[1, j].astype(BF)
    for j in range(NCH):
        to_y[j].wait_send()
        to_c[j].wait_send()
        pass_c[j].wait_send()


def rest_of_step(o, st, hidden, g2, g3, qn, g4, gates, mask, xvalid, ws, k_cross, v_cross):
    wo, wg, wu, wd, wq, wo2 = ws[:6]
    F = wg.shape[1]
    T2 = k_cross.shape[1]
    dma = pltpu.SemaphoreType.DMA
    sum_bufs = [pltpu.VMEM((NCH, NQ, W), F32)] * 4 + [dma((4, NCH))]
    share_bufs = [pltpu.VMEM((NQ, HID), F32)] * 2 + [dma((2,))]
    return pl.pallas_call(
        rest_kernel,
        in_specs=[ANY, VM, ANY, VM, VM, VM, VM, pl.BlockSpec(memory_space=pltpu.SMEM), VM] + [ANY] * 12,
        out_specs=VM,
        out_shape=jax.ShapeDtypeStruct((NB, HID), BF),
        scratch_shapes=[pltpu.VMEM(w.shape, BF) for w in (wo, wg, wu, wd, wq, wo2)] + [
            dma((10,)), pltpu.VMEM((NR, CR, T2, D), BF), pltpu.VMEM((NR, CR, T2, D), BF), dma((2, NR)),
            pltpu.VMEM((NH * HL, D), F32), pltpu.VMEM((NH * HL, D), F32), pltpu.VMEM((8, D), F32),
            pltpu.VMEM((8, D), F32), dma((4,)), pltpu.VMEM((NQ, HID), BF), pltpu.VMEM((NH * HL, D), F32),
            pltpu.VMEM((NH, xvalid.shape[1]), jnp.int32), pltpu.VMEM((NH, D), jnp.int32),
            pltpu.VMEM((NH * 8, D), F32), pltpu.VMEM((NH, HID), BF), pltpu.VMEM((NH, F), BF),
            pltpu.VMEM((NQ, HID), BF), pltpu.VMEM((NQ, HID), BF), pltpu.VMEM((NCH, NQ, W), F32),
            pltpu.VMEM((NCH, NQ, W), F32), pltpu.VMEM((2, NCH, NQ, W), F32), dma((6, NCH))]
        + sum_bufs + sum_bufs + [pltpu.VMEM((NCH, RC, HID), F32)] * 4 + [dma((4, NCH)), dma((2, NCH))]
        + share_bufs + share_bufs + [dma((4, NCH))],
        compiler_params=pltpu.CompilerParams(collective_id=0, has_side_effects=True, vmem_limit_bytes=VMEM_MAX),
        name="rest_of_step",
    )(o, st, hidden, g2, g3, qn, g4, gates, mask, xvalid, *ws, k_cross, v_cross)


def solution(mesh):
    cache_spec = P('dp', 'sp', 'tp', None)
    cross_spec = P('dp', None, 'tp', None)
    row_spec = P('dp', None)
    vec_spec = P('dp')
    full_spec = P(None)
    col_spec = P(None, 'tp')
    split_rows = P('tp', None)
    in_specs = (row_spec, vec_spec, cache_spec, cache_spec, cross_spec, cross_spec, row_spec, vec_spec,
                full_spec, col_spec, col_spec, col_spec, split_rows, full_spec, col_spec, col_spec, split_rows,
                full_spec, col_spec, full_spec, split_rows, full_spec, full_spec, col_spec, col_spec, split_rows)
    out_specs = (row_spec, cache_spec, cache_spec)

    def local_step(hidden, new_pos, k_self, v_self, k_cross, v_cross, xvalid, rowmask,
                   self_attn_norm, self_wq, self_wk, self_wv, self_wo, self_mlp_norm,
                   self_wgate, self_wup, self_wdown, cross_attn_norm, cross_wq, cross_qnorm,
                   cross_wo, cross_gates, cross_mlp_norm, cross_wgate, cross_wup, cross_wdown):
        flat = lambda a: a.reshape(a.shape[0], a.shape[1] * a.shape[2], a.shape[3])
        k_out, v_out, o, st = self_attention(new_pos, self_attn_norm, hidden, self_wq, self_wk, self_wv,
                                             flat(k_self), flat(v_self))
        weights = (self_wo, self_wgate, self_wup, self_wdown, cross_wq, cross_wo, cross_wgate, cross_wup, cross_wdown)
        h4 = rest_of_step(o, st, hidden, self_mlp_norm, cross_attn_norm, cross_qnorm, cross_mlp_norm, cross_gates,
                          rowmask, xvalid, weights, flat(k_cross), flat(v_cross))
        return h4, k_out.reshape(k_self.shape), v_out.reshape(v_self.shape)

    return jax.shard_map(local_step, mesh=mesh, in_specs=in_specs, out_specs=out_specs, check_vma=False)
```

time: 184 us -> 130 us (0.71)
  Pallas kernels: 170 us -> 126 us
  local copies, waits for them, and re-layouts: 8.25 us -> 2.3 us
  other arithmetic: 5.23 us -> 0 us
    pallas_call x4 -> x2, Pallas kernels: 170 us -> 126 us  [the longest x1 98.3 us: rest_of_step(): pl.pallas_call(rest_kernel, in_specs=[ANY, VM, ANY, VM, VM, VM, VM, pl.Bl...]
    reshape x4 -> x0, local copies, waits for them, and re-layouts: 5.14 us -> none  [local_step(): row = lambda a: a.reshape(1, -1)]
    convert_element_type x2 -> x0, other arithmetic: 2.02 us -> none  [the longest x1 1.34 us: local_step(): angles = new_pos.astype(F32)[:, None] * rope_freqs(D)[None, :]]
where the time goes in v2:
time: 130 us; the launch traced here: 129 us
  Pallas kernels  126 us (97%)
  local copies, waits for them, and re-layouts  2.3 us (2%)
    pallas_call x1, Pallas kernels, rest_of_step(): pl.pallas_call(rest_kernel, in_specs=[ANY, VM, ANY, VM, VM, VM, VM, pl.Bl...  98.3 us
    pallas_call x1, Pallas kernels, self_attention(): pl.pallas_call(self_kernel, in_specs=[pl.BlockSpec(memory_space=pltpu.SME...  28.1 us

profile of v2, /device:TPU:0, one launch (start us, length us, event | category | flops | bytes accessed | tf_op | source)
XLA Modules:
  0.0 129.3 jit_solution(3668163249869884740)
XLA Ops:
  0.6 28.1 %self_attn.1 = (bf16[256,256,128]{2,1,0:T(8,128)(2,1)}, bf16[256,256,128]{2,1,0:T(8,128)(2,1)}, f32[1024,128]{1,0:T(8,128)}, f32[16,128]{1,0:T(8,128)}) custom-call(s32[256]{0:T(256)} %posv_ref.1, s32[256]{0:T(256)} %posv_ref.1, f32[1,128]{1,0:T(1,128)} %constant.2.clone.freq_ref, bf16[2048]{0:T(1024)(128)(2,1)} %g_ref.1, bf16[256,2048]{1,0:T(8,128)(2,1)} %hid_hbm.3, ...), custom_call_target="tpu_custom_call" | custom-call | tf_op jit(solution)/shard_map/self_attn/pallas_call | solution.py:197
  28.7 98.3 %rest_of_step.1 = bf16[256,2048]{1,0:T(8,128)(2,1)} custom-call(f32[1024,128]{1,0:T(8,128)} %get-tuple-element.7.o_hbm, f32[16,128]{1,0:T(8,128)} %get-tuple-element.8.st_ref, bf16[256,2048]{1,0:T(8,128)(2,1)} %hid_hbm.3, bf16[2048]{0:T(1024)(128)(2,1)} %g2_ref.1, bf16[2048]{0:T(1024)(128)(2,1)} %g3_ref.1, bf16[128]{0:T(256)(128)(2,1)} %qn_ref.1, ...), custom_call_target="tpu_custom_call" | custom-call | tf_op jit(solution)/shard_map/rest_of_step/pallas_call | solution.py:492
  127.0 2.3 %copy.31 = bf16[256,2048]{1,0:T(8,128)(2,1)} copy(bf16[256,2048]{1,0:T(8,128)(2,1)} %rest_of_step.1) | data formatting | bytes 2097152

commit v3 on v2

--- a/solution.py
+++ b/solution.py
@@ -25,6 +25,7 @@
 NH = 128
 NQ = 64
 HID = 2048
+HQ = NQ // 2
 NCH = 4
 W = HID // NCH
 VMEM_MAX = 66 * 1024 * 1024 - 2 * 1024 * 1024
@@ -228,34 +229,49 @@
                                         device_id=dev, device_id_type=MESH)
 
 
-def tp_sum(pe, compute, finish, snd, rcv, chip, xr, sems):
-    to_core = [rcopy(snd.at[j], rcv.at[j], sems.at[0, j], sems.at[1, j], pe["c"]) for j in range(NCH)]
-    to_chip = [rcopy(chip.at[j], xr.at[j], sems.at[2, j], sems.at[3, j], pe["x"]) for j in range(NCH)]
-    for j in range(NCH + 1):
-        if j < NCH:
-            part = compute(j)
-            snd[j] = part[NQ:]
-            chip[j] = part[:NQ]
-            to_core[j].start()
-        if j >= 1:
-            to_core[j - 1].wait_recv()
-            chip[j - 1] = chip[j - 1] + rcv[j - 1]
-            to_chip[j - 1].start()
-    for j in range(NCH):
-        to_chip[j].wait_recv()
-        finish(j, chip[j] + xr[j])
-    for j in range(NCH):
-        to_core[j].wait_send()
-        to_chip[j].wait_send()
-
-
-def share_rows(pe, own, x_ref, snd, rcv, sem):
-    snd[...] = own.astype(F32)
-    cp = rcopy(snd, rcv, sem.at[0], sem.at[1], pe["c"])
-    cp.start()
-    x_ref[pl.ds(0, NQ), :] = own
-    cp.wait()
-    x_ref[pl.ds(NQ, NQ), :] = rcv[...].astype(BF)
+class TpSum:
+    def __init__(self, pe, half, bufs):
+        snd, rcv, chip, xr, sems = bufs
+        self.snd, self.rcv, self.chip, self.xr = (b.at[half] for b in (snd, rcv, chip, xr))
+        at = lambda n, j: sems.at[half, n, j]
+        self.to_core = [rcopy(self.snd.at[j], self.rcv.at[j], at(0, j), at(1, j), pe["c"]) for j in range(NCH)]
+        self.to_chip = [rcopy(self.chip.at[j], self.xr.at[j], at(2, j), at(3, j), pe["x"]) for j in range(NCH)]
+
+    def start(self, compute):
+        for j in range(NCH + 1):
+            if j < NCH:
+                part = compute(j)
+                self.snd[j] = part[HQ:]
+                self.chip[j] = part[:HQ]
+                self.to_core[j].start()
+            if j >= 1:
+                self.to_core[j - 1].wait_recv()
+                self.chip[j - 1] = self.chip[j - 1] + self.rcv[j - 1]
+                self.to_chip[j - 1].start()
+
+    def close(self, finish):
+        for j in range(NCH):
+            self.to_chip[j].wait_recv()
+            finish(j, self.chip[j] + self.xr[j])
+        for j in range(NCH):
+            self.to_core[j].wait_send()
+            self.to_chip[j].wait_send()
+
+
+class Share:
+    def __init__(self, pe, half, x_ref, snd, rcv, sems):
+        rows = pl.ds(half * HQ, HQ)
+        self.snd, self.rcv, self.x = snd.at[rows], rcv.at[rows], x_ref.at[half]
+        self.copy = rcopy(self.snd, self.rcv, sems.at[0, half], sems.at[1, half], pe["c"])
+
+    def start(self, own):
+        self.snd[...] = own.astype(F32)
+        self.copy.start()
+        self.x[pl.ds(0, HQ), :] = own
+
+    def finish(self):
+        self.copy.wait()
+        self.x[pl.ds(HQ, HQ), :] = self.rcv[...].astype(BF)
 
 
 def mlp_act(x_ref, wg, wu, act, n_cols):
@@ -322,10 +338,16 @@
     mine = jnp.where(sp == 0, both[:8], both[8:])
     sts[...] = jnp.where(sp == 0, both[8:], both[:8])
     local[0].wait()
-    cp_o = rcopy(osnd, orcv, ysem.at[0], ysem.at[1], pe["y"])
-    cp_s = rcopy(sts, str_, ysem.at[2], ysem.at[3], pe["y"])
+    cp_s = rcopy(sts, str_, ysem.at[0, 4], ysem.at[1, 4], pe["y"])
     cp_s.start()
-    cp_o.start()
+
+    def quarter(h, c):
+        rows = pl.ds((c * NQ + h * HQ) * HL, HQ * HL)
+        return rcopy(osnd.at[rows], orcv.at[rows], ysem.at[0, 2 * h + c], ysem.at[1, 2 * h + c], pe["y"])
+
+    quarters = [quarter(h, c) for h in range(2) for c in range(2)]
+    for cp in quarters:
+        cp.start()
     for cp in local[1:]:
         cp.wait()
     some = jnp.sum((valid[...] > 0).astype(jnp.int32), axis=1, keepdims=True)
@@ -333,47 +355,74 @@
     row_scale = column(mask_ref[...].astype(F32).reshape(1, NB), sp * NH + core * NQ, NQ)
     gate0 = jnp.tanh(jnp.full((8, D), gates_ref[0], F32))[0:1, 0:1] * row_scale
     gate1 = jnp.tanh(jnp.full((8, D), gates_ref[1], F32))[0:1, 0:1] * row_scale
+    gain = lambda ref: ref[...].astype(F32).reshape(1, HID)
+    owned = [slice(h * HQ, (h + 1) * HQ) for h in range(2)]
+    sum1 = [TpSum(pe, h, (a0, a1, a2, a3, asem)) for h in range(2)]
+    sum2 = [TpSum(pe, h, (b0, b1, b2, b3, bsem)) for h in range(2)]
+    sum4 = [TpSum(pe, h, (a0, a1, a2, a3, esem)) for h in range(2)]
+    share1 = [Share(pe, h, xbuf, s0, s1, ssem) for h in range(2)]
+    share2 = [Share(pe, h, xbuf, t0, t1, tsem) for h in range(2)]
+
     cp_s.wait()
     theirs = str_[...]
     top = jnp.maximum(mine, theirs)
     f1, f2 = jnp.exp(mine - top), jnp.exp(theirs - top)
     den = pltpu.roll(mine, NQ, 1) * f1 + pltpu.roll(theirs, NQ, 1) * f2
     w1, w2 = f1 / den, f2 / den
-    cp_o.wait()
-    for p in range(NQ):
-        s = pl.ds(8 * p, 8)
-        att[s, :] = att[s, :] * w1[:, p:p + 1] + orcv[s, :] * w2[:, p:p + 1]
-    lhs = heads_to_lanes(att, (core * NQ, (1 - core) * NQ), NQ)
-    gain = lambda ref: ref[...].astype(F32).reshape(1, HID)
+
+    def attn_out(h):
+        for c in range(2):
+            quarters[2 * h + c].wait()
+            for p in range((c * NQ + h * HQ) // 2, (c * NQ + h * HQ + HQ) // 2):
+                s = pl.ds(8 * p, 8)
+                att[s, :] = att[s, :] * w1[:, p:p + 1] + orcv[s, :] * w2[:, p:p + 1]
+        lhs = heads_to_lanes(att, (core * NQ + h * HQ, (1 - core) * NQ + h * HQ), HQ)
+        sum1[h].start(lambda j: dot(lhs, wo[:, cols(j)]))
+
+    def close1(h):
+        def done(j, total):
+            hres[owned[h], cols(j)] = (hown[owned[h], cols(j)].astype(F32) + total).astype(BF)
+
+        sum1[h].close(done)
+        share1[h].start(norm32(hres[owned[h], :].astype(F32), gain(g2_ref)))
+
+    def mlp(h, total):
+        mlp_act(xbuf.at[h], wg, wu, act.at[h], act.shape[2])
+        total.start(lambda j: dot(act[h], wd[:, cols(j)]))
+
+    def close2(h):
+        def done(j, total):
+            h2[owned[h], cols(j)] = (hres[owned[h], cols(j)].astype(F32) + total).astype(BF)
+
+        sum2[h].close(done)
+        share2[h].start(norm32(h2[owned[h], :].astype(F32), gain(g3_ref)))
+
+    def cross_q(h):
+        share2[h].finish()
+        q = dot(xbuf[h], wq[...])
+        qgain = qn_ref[...].astype(F32).reshape(1, D)
+        heads = [norm32(q[:, n * D:(n + 1) * D].astype(BF).astype(F32), qgain).astype(F32) for n in range(HL)]
+        spread_heads(qx, [x[:HQ] for x in heads], core * NQ + h * HQ, HQ)
+        spread_heads(qx, [x[HQ:] for x in heads], (1 - core) * NQ + h * HQ, HQ)
 
     loads[0].wait()
-
-    def done1(j, total):
-        hres[:, cols(j)] = (hown[:, cols(j)].astype(F32) + total).astype(BF)
-
-    tp_sum(pe, lambda j: dot(lhs, wo[:, cols(j)]), done1, a0, a1, a2, a3, asem)
-    share_rows(pe, norm32(hres[...].astype(F32), gain(g2_ref)), xbuf, s0, s1, ssem)
-    loads[1].wait()
-    loads[2].wait()
-    mlp_act(xbuf, wg, wu, act, act.shape[1])
-    loads[3].wait()
-
-    def done2(j, total):
-        if j == 0:
-            for cp in loads2:
-                cp.start()
-        h2[:, cols(j)] = (hres[:, cols(j)].astype(F32) + total).astype(BF)
-
+    attn_out(0)
+    attn_out(1)
+    close1(0)
+    share1[0].finish()
+    for cp in loads[1:4]:
+        cp.wait()
+    mlp(0, sum2[0])
+    close1(1)
+    share1[1].finish()
+    mlp(1, sum2[1])
     loads2 = [pltpu.make_async_copy(a, b, wsem.at[1 + n])
               for n, (a, b) in enumerate(((wg2_hbm, wg), (wu2_hbm, wu), (wd2_hbm, wd)))]
-    tp_sum(pe, lambda j: dot(act[...], wd[:, cols(j)]), done2, b0, b1, b2, b3, bsem)
-    share_rows(pe, norm32(h2[...].astype(F32), gain(g3_ref)), xbuf, t0, t1, tsem)
+    for cp in loads2:
+        cp.start()
+    close2(0)
     loads[4].wait()
-    q = dot(xbuf[...], wq[...])
-    qgain = qn_ref[...].astype(F32).reshape(1, D)
-    heads = [norm32(q[:, h * D:(h + 1) * D].astype(BF).astype(F32), qgain).astype(F32) for h in range(HL)]
-    spread_heads(qx, [h[:NQ] for h in heads], core * NQ, NQ)
-    spread_heads(qx, [h[NQ:] for h in heads], (1 - core) * NQ, NQ)
+    cross_q(0)
     loads[5].wait()
 
     col = lax.broadcasted_iota(jnp.int32, (8, T2), 1)
@@ -413,73 +462,109 @@
         c2[j] = c2[j] + c1[j]
         to_chip[j].start()
 
-    def close(j):
+    def close3(j):
         mine = slice(j * RC, (j + 1) * RC)
         to_chip[j].wait_recv()
         hres[mine, :] = (h2[mine, :].astype(F32) + gate0[mine] * (c2[j] + c3[j])).astype(BF)
         own = norm32(hres[mine, :].astype(F32), gain(g4_ref))
         s0[mine, :] = own.astype(F32)
         share[j].start()
-        xbuf[mine, :] = own
-
-    for j in range(NCH):
-        lax.fori_loop(j * XB, j * XB + 1, block, 0)
-        if j >= 1:
-            pass_chip(j - 1)
-        lax.fori_loop(j * XB + 1, (j + 1) * XB, block, 0)
+        xbuf[j // 2, pl.ds((j % 2) * RC, RC), :] = own
+
+    def shared3(j):
+        share[j].wait_recv()
+        xbuf[j // 2, pl.ds(HQ + (j % 2) * RC, RC), :] = s1[pl.ds(j * RC, RC), :].astype(BF)
+
+    def cross_out(j):
         lhs = heads_to_lanes(att, (core * NQ + j * RC, (1 - core) * NQ + j * RC), RC)
         for n in range(NCH):
             part = dot(lhs, wo2[:, cols(n)])
             c0[j, :, cols(n)] = part[RC:]
             c2[j, :, cols(n)] = part[:RC]
         to_core[j].start()
-        if j >= 1:
-            close(j - 1)
-    pass_chip(NCH - 1)
-    close(NCH - 1)
+
+    to_y = [[rcopy(fin.at[h, j], yr.at[h, j], gsem.at[h, 0, j], gsem.at[h, 1, j], pe["y"]) for j in range(NCH)]
+            for h in range(2)]
+    to_c = [[rcopy(fin.at[h, j], cr.at[0, h, j], gsem.at[h, 2, j], gsem.at[h, 3, j], pe["c"]) for j in range(NCH)]
+            for h in range(2)]
+    pass_c = [[rcopy(yr.at[h, j], cr.at[1, h, j], gsem.at[h, 4, j], gsem.at[h, 5, j], pe["c"]) for j in range(NCH)]
+              for h in range(2)]
+
+    def rows(of_sp, of_core, h):
+        return pl.ds(pl.multiple_of(of_sp * NH + of_core * NQ + h * HQ, HQ), HQ)
+
+    def pass_on(h, j):
+        to_y[h][j].wait_recv()
+        pass_c[h][j].start()
+
+    def close4(h, passing):
+        def done(j, total):
+            res = (hres[owned[h], cols(j)].astype(F32) + gate1[owned[h]] * total).astype(BF)
+            out_ref[rows(sp, core, h), cols(j)] = res
+            fin[h, j] = res.astype(F32)
+            to_y[h][j].start()
+            to_c[h][j].start()
+            if passing and j >= 1:
+                pass_on(h, j - 1)
+
+        sum4[h].close(done)
+
+    def gathered(h):
+        for j in range(NCH):
+            out_ref[rows(1 - sp, core, h), cols(j)] = yr[h, j].astype(BF)
+            to_c[h][j].wait_recv()
+            out_ref[rows(sp, 1 - core, h), cols(j)] = cr[0, h, j].astype(BF)
+        for j in range(NCH):
+            pass_c[h][j].wait_recv()
+            out_ref[rows(1 - sp, 1 - core, h), cols(j)] = cr[1, h, j].astype(BF)
+        for j in range(NCH):
+            to_y[h][j].wait_send()
+            to_c[h][j].wait_send()
+            pass_c[h][j].wait_send()
+
+    blocks_to = lambda lo, hi: lax.fori_loop(lo, hi, block, 0)
+    blocks_to(0, 4)
+    cross_out(0)
+    blocks_to(4, 5)
+    pass_chip(0)
+    blocks_to(5, 7)
+    close2(1)
+    blocks_to(7, 8)
+    cross_out(1)
+    cross_q(1)
+    blocks_to(8, 9)
+    pass_chip(1)
+    close3(0)
+    blocks_to(9, 12)
+    cross_out(2)
+    blocks_to(12, 13)
+    pass_chip(2)
+    close3(1)
+    blocks_to(13, 15)
+    shared3(0)
+    shared3(1)
+    for cp in loads2:
+        cp.wait()
+    mlp(0, sum4[0])
+    blocks_to(15, 16)
+    cross_out(3)
+    close3(2)
+    pass_chip(3)
+    close4(0, False)
+    close3(3)
     for j in range(NCH):
-        share[j].wait_recv()
-        xbuf[pl.ds(NQ + j * RC, RC), :] = s1[pl.ds(j * RC, RC), :].astype(BF)
+        pass_on(0, j)
+    shared3(2)
+    shared3(3)
+    mlp(1, sum4[1])
+    gathered(0)
+    close4(1, True)
+    pass_on(1, NCH - 1)
+    gathered(1)
     for j in range(NCH):
         to_core[j].wait_send()
         to_chip[j].wait_send()
         share[j].wait_send()
-    for cp in loads2[:2]:
-        cp.wait()
-    mlp_act(xbuf, wg, wu, act, act.shape[1])
-    loads2[2].wait()
-
-    to_y = [rcopy(fin.at[j], yr.at[j], gsem.at[0, j], gsem.at[1, j], pe["y"]) for j in range(NCH)]
-    to_c = [rcopy(fin.at[j], cr.at[0, j], gsem.at[2, j], gsem.at[3, j], pe["c"]) for j in range(NCH)]
-    pass_c = [rcopy(yr.at[j], cr.at[1, j], gsem.at[4, j], gsem.at[5, j], pe["c"]) for j in range(NCH)]
-
-    def rows(of_half, of_core):
-        return pl.ds(pl.multiple_of(of_half * NH + of_core * NQ, NQ), NQ)
-
-    def done4(j, total):
-        res = (hres[:, cols(j)].astype(F32) + gate1 * total).astype(BF)
-        out_ref[rows(sp, core), cols(j)] = res
-        fin[j] = res.astype(F32)
-        to_y[j].start()
-        to_c[j].start()
-        if j >= 1:
-            to_y[j - 1].wait_recv()
-            pass_c[j - 1].start()
-
-    tp_sum(pe, lambda j: dot(act[...], wd[:, cols(j)]), done4, a0, a1, a2, a3, esem)
-    to_y[NCH - 1].wait_recv()
-    pass_c[NCH - 1].start()
-    for j in range(NCH):
-        out_ref[rows(1 - sp, core), cols(j)] = yr[j].astype(BF)
-        to_c[j].wait_recv()
-        out_ref[rows(sp, 1 - core), cols(j)] = cr[0, j].astype(BF)
-    for j in range(NCH):
-        pass_c[j].wait_recv()
-        out_ref[rows(1 - sp, 1 - core), cols(j)] = cr[1, j].astype(BF)
-    for j in range(NCH):
-        to_y[j].wait_send()
-        to_c[j].wait_send()
-        pass_c[j].wait_send()
 
 
 def rest_of_step(o, st, hidden, g2, g3, qn, g4, gates, mask, xvalid, ws, k_cross, v_cross):
@@ -487,8 +572,8 @@
     F = wg.shape[1]
     T2 = k_cross.shape[1]
     dma = pltpu.SemaphoreType.DMA
-    sum_bufs = [pltpu.VMEM((NCH, NQ, W), F32)] * 4 + [dma((4, NCH))]
-    share_bufs = [pltpu.VMEM((NQ, HID), F32)] * 2 + [dma((2,))]
+    sum_bufs = [pltpu.VMEM((2, NCH, HQ, W), F32)] * 4 + [dma((2, 4, NCH))]
+    share_bufs = [pltpu.VMEM((NQ, HID), F32)] * 2 + [dma((2, 2))]
     return pl.pallas_call(
         rest_kernel,
         in_specs=[ANY, VM, ANY, VM, VM, VM, VM, pl.BlockSpec(memory_space=pltpu.SMEM), VM] + [ANY] * 12,
@@ -497,13 +582,13 @@
         scratch_shapes=[pltpu.VMEM(w.shape, BF) for w in (wo, wg, wu, wd, wq, wo2)] + [
             dma((10,)), pltpu.VMEM((NR, CR, T2, D), BF), pltpu.VMEM((NR, CR, T2, D), BF), dma((2, NR)),
             pltpu.VMEM((NH * HL, D), F32), pltpu.VMEM((NH * HL, D), F32), pltpu.VMEM((8, D), F32),
-            pltpu.VMEM((8, D), F32), dma((4,)), pltpu.VMEM((NQ, HID), BF), pltpu.VMEM((NH * HL, D), F32),
+            pltpu.VMEM((8, D), F32), dma((2, 5)), pltpu.VMEM((NQ, HID), BF), pltpu.VMEM((NH * HL, D), F32),
             pltpu.VMEM((NH, xvalid.shape[1]), jnp.int32), pltpu.VMEM((NH, D), jnp.int32),
-            pltpu.VMEM((NH * 8, D), F32), pltpu.VMEM((NH, HID), BF), pltpu.VMEM((NH, F), BF),
-            pltpu.VMEM((NQ, HID), BF), pltpu.VMEM((NQ, HID), BF), pltpu.VMEM((NCH, NQ, W), F32),
-            pltpu.VMEM((NCH, NQ, W), F32), pltpu.VMEM((2, NCH, NQ, W), F32), dma((6, NCH))]
+            pltpu.VMEM((NH * 8, D), F32), pltpu.VMEM((2, NQ, HID), BF), pltpu.VMEM((2, NQ, F), BF),
+            pltpu.VMEM((NQ, HID), BF), pltpu.VMEM((NQ, HID), BF), pltpu.VMEM((2, NCH, HQ, W), F32),
+            pltpu.VMEM((2, NCH, HQ, W), F32), pltpu.VMEM((2, 2, NCH, HQ, W), F32), dma((2, 6, NCH))]
         + sum_bufs + sum_bufs + [pltpu.VMEM((NCH, RC, HID), F32)] * 4 + [dma((4, NCH)), dma((2, NCH))]
-        + share_bufs + share_bufs + [dma((4, NCH))],
+        + share_bufs + share_bufs + [dma((2, 4, NCH))],
         compiler_params=pltpu.CompilerParams(collective_id=0, has_side_effects=True, vmem_limit_bytes=VMEM_MAX),
         name="rest_of_step",
     )(o, st, hidden, g2, g3, qn, g4, gates, mask, xvalid, *ws, k_cross, v_cross)

time: 130 us -> 119 us (0.915)
  Pallas kernels: 126 us -> 116 us
    pallas_call x1, Pallas kernels: 98.3 us -> 88 us  [rest_of_step(): pl.pallas_call(rest_kernel, in_specs=[ANY, VM, ANY, VM, VM, VM, VM, pl.Bl...]
where the time goes in v3:
time: 119 us
  Pallas kernels  116 us (97%)
  local copies, waits for them, and re-layouts  2.3 us (2%)
    pallas_call x1, Pallas kernels, rest_of_step(): pl.pallas_call(rest_kernel, in_specs=[ANY, VM, ANY, VM, VM, VM, VM, pl.Bl...  88 us
    pallas_call x1, Pallas kernels, self_attention(): pl.pallas_call(self_kernel, in_specs=[pl.BlockSpec(memory_space=pltpu.SME...  28.1 us

profile of v3, /device:TPU:0, one launch (start us, length us, event | category | flops | bytes accessed | tf_op | source)
XLA Modules:
  0.0 119.1 jit_solution(6535363293674225659)
XLA Ops:
  0.6 28.1 %self_attn.1 = (bf16[256,256,128]{2,1,0:T(8,128)(2,1)}, bf16[256,256,128]{2,1,0:T(8,128)(2,1)}, f32[1024,128]{1,0:T(8,128)}, f32[16,128]{1,0:T(8,128)}) custom-call(s32[256]{0:T(256)} %posv_ref.1, s32[256]{0:T(256)} %posv_ref.1, f32[1,128]{1,0:T(1,128)} %constant.2.clone.freq_ref, bf16[2048]{0:T(1024)(128)(2,1)} %g_ref.1, bf16[256,2048]{1,0:T(8,128)(2,1)} %hid_hbm.3, ...), custom_call_target="tpu_custom_call" | custom-call | tf_op jit(solution)/shard_map/self_attn/pallas_call | solution.py:198
  28.7 88.0 %rest_of_step.1 = bf16[256,2048]{1,0:T(8,128)(2,1)} custom-call(f32[1024,128]{1,0:T(8,128)} %get-tuple-element.7.o_hbm, f32[16,128]{1,0:T(8,128)} %get-tuple-element.8.st_ref, bf16[256,2048]{1,0:T(8,128)(2,1)} %hid_hbm.3, bf16[2048]{0:T(1024)(128)(2,1)} %g2_ref.1, bf16[2048]{0:T(1024)(128)(2,1)} %g3_ref.1, bf16[128]{0:T(256)(128)(2,1)} %qn_ref.1, ...), custom_call_target="tpu_custom_call" | custom-call | tf_op jit(solution)/shard_map/rest_of_step/pallas_call | solution.py:577
  116.8 2.3 %copy.31 = bf16[256,2048]{1,0:T(8,128)(2,1)} copy(bf16[256,2048]{1,0:T(8,128)(2,1)} %rest_of_step.1) | data formatting | bytes 2097152
